TPU v7x, 256 devices: a whole 4x4x8 slice. The times are simulated.
256 devices in a mesh: leaf: 256 (over y, x, z, core).
Axes of the slice: x: 4, y: 4, z: 8, core: 2. Of those that a mesh axis runs over, the one named last changes fastest.
Arguments:
- points: bfloat16 [262144, 512], P('leaf'), may hold values from -6 to 6
- weights: float32 [262144, 64], P('leaf'), may hold values from -6 to 6
- leaf_basis: float32 [262144, 256], P('leaf'), may hold values from -0.1875 to 0.1875
- transfer: float32 [256, 7, 256, 256], P('leaf'), may hold values from -0.375 to 0.375
- skeleton_index: int32 [8, 256, 256], replicated, may hold values from 0 to 1023, as said below
- node_owner: int32 [6, 256], replicated, may hold values from 0 to 63, as said below
- near_list: int32 [256, 3], replicated, may hold values from 0 to 7, as said below
Outputs:
- product: float32 [262144, 64], P('leaf')
Inputs may be any that keep to these rules, and one draw needn't show every extreme that they name: `near_list`: entry m > 0 of row i names leaf i XOR m of the same aligned group of 8 leaves; 0 marks an empty slot. The nonzero entries of a row are distinct and number 1 to 3; some row has 3. `skeleton_index`: row 0, column i: 256 distinct row numbers below 1024 within leaf i. Row m >= 1, column s below 256 >> m: 256 distinct row numbers below 512; other columns are unused. `node_owner`: row m - 1, column s below 256 >> m: a number below 2 to the power m; other columns are unused.
All inputs are finite; a program needn't handle non-finite values.
Results may differ from a plain program's by a relative error of at most 0.0018.
Values may be sent and summed in bfloat16 or wider, within the bound.
No kernel may reach another device: no remote copies, remote signals or barrier semaphores. Data moves between devices by JAX's collectives and lax.ppermute only.
A program may use at most 128 MiB of HBM per device.

v0:
```python
import jax
import jax.numpy as jnp
from jax import lax
from jax.experimental import pallas as pl
from jax.experimental.pallas import tpu as pltpu
from jax.sharding import PartitionSpec as P


GROUP = 8
PTS = 1024
DIM = 512
RANK = 256
RHS = 64
ROWS = PTS + 4 * RHS + RHS
SCALE = 2.0 / DIM
INTERPRET = False

BITS = 0
CORE = 0
OWNED = 8
KIND = 16
SIDE = 32
FARKIND = 33
BEYOND = 40

F32 = jnp.float32
BF16 = jnp.bfloat16
NN = (((1,), (0,)), ((), ()))
NT = (((1,), (1,)), ((), ()))


def mm(a, b, dims=NN):
    return lax.dot_general(a, b, dims, preferred_element_type=F32)


def split(a):
    high = a.astype(BF16)
    return high, (a - high.astype(F32)).astype(BF16)


def product(a, b, dims=NN):
    a_high, a_low = split(a)
    b_high, b_low = split(b)
    rows = a.shape[0]
    both = mm(jnp.concatenate([a_high, a_low], 0), b_high, dims)
    return both[:rows] + both[rows:] + mm(a_high, b_low, dims)


def row_norms(rows):
    wide = rows.astype(F32)
    high, low = split(wide * wide)
    ones = jnp.ones((8, rows.shape[1]), BF16)
    return mm(ones, high, NT) + mm(ones, low, NT)


def kern(left, right, right_norm):
    wide = left.astype(F32)
    left_norm = jnp.sum(wide * wide, axis=1, keepdims=True)
    inner = mm(left, right, NT)
    return jnp.exp(-SCALE * (left_norm + right_norm - 2.0 * inner))


def pick_matrix(picks, count):
    lanes = lax.broadcasted_iota(jnp.int32, (picks.shape[0], count), 1)
    return jnp.where(lanes == picks, 1.0, 0.0).astype(BF16)


def weighted(values, block):
    half = values.shape[0] // 2
    high, low = split(block)
    both = mm(values, high)
    return both[:half] + both[half:] + mm(values[:half], low)


def call(body, outs, args, smem=0, flops=0, far=0, scratch=()):
    near = len(args) - far
    in_specs = [
        pl.BlockSpec(memory_space=pltpu.SMEM if k < smem else pltpu.VMEM if k < near else pltpu.HBM)
        for k in range(len(args))
    ]
    size = sum(a.size * a.dtype.itemsize for a in args)
    return pl.pallas_call(
        body,
        out_shape=[jax.ShapeDtypeStruct(s, d) for s, d in outs],
        in_specs=in_specs,
        out_specs=[pl.BlockSpec(memory_space=pltpu.VMEM) for _ in outs],
        scratch_shapes=list(scratch),
        compiler_params=pltpu.CompilerParams(vmem_limit_bytes=40 << 20),
        cost_estimate=pl.CostEstimate(flops=flops, transcendentals=0, bytes_accessed=size),
        interpret=INTERPRET,
    )(*args)


def lift(values, pair):
    high, low = split(values)
    rows = values.shape[0]
    both = mm(jnp.concatenate([high, low], 0), pair[:, :RANK])
    return both[:rows] + both[rows:] + mm(high, pair[:, RANK:])


def lower(values, pair):
    high, low = split(values)
    rows = values.shape[0]
    both = mm(jnp.concatenate([high, low], 0), pair[:, :RANK], NT)
    return both[:rows] + both[rows:] + mm(high, pair[:, RANK:], NT)


def pack(values):
    high, low = split(values)
    return jnp.concatenate([high, low], 1)


def unpack(pair):
    return pair[:, :RANK].astype(F32) + pair[:, RANK:].astype(F32)


def prepare_body(x_ref, b_ref, v_ref, p_ref, w_ref):
    b_high, b_low = split(b_ref[...])
    v_high, v_low = split(v_ref[...])
    both = mm(jnp.concatenate([b_high, b_low], 0), v_high)
    w = both[:RHS] + both[RHS:] + mm(b_high, v_low)
    w_ref[...] = w
    p_ref[0:PTS, :] = x_ref[...]
    for k, part in enumerate((b_high[:, :DIM], b_low[:, :DIM], b_high[:, DIM:], b_low[:, DIM:])):
        p_ref[PTS + k * RHS : PTS + (k + 1) * RHS, :] = part
    p_ref[PTS + 4 * RHS :, :] = pack(w)


def skeleton_body(flag_ref, both_ref, col_ref, z_ref, nz_ref, nx_ref, rows_ref):
    for k in range(2):
        x = both_ref[k * ROWS : k * ROWS + PTS, :]
        z = mm(pick_matrix(col_ref[:, 8 + k : 9 + k], PTS), x).astype(BF16)
        z_ref[k] = z
        nz_ref[k] = row_norms(z)
        nx_ref[k] = row_norms(x)
    upper = flag_ref[BITS] * RANK
    picks = col_ref[:, 1:2]
    rows = mm(pick_matrix(picks - upper, RANK), z_ref[0]) + mm(pick_matrix(picks - (RANK - upper), RANK), z_ref[1])
    rows_ref[...] = rows.astype(BF16)


def add_near(source, x, norm, near_ref, place):
    p_ref, top = source

    def step(k, carry):
        for h in range(2):
            first = pl.multiple_of(top + k * 512 + h * 256, 16)
            block = kern(p_ref[pl.ds(first, 256), :], x, norm)
            row = pl.multiple_of(top + PTS + k * (2 * RHS), 16)
            values = p_ref[pl.ds(row, 2 * RHS), h * 256 : (h + 1) * 256]
            near_ref[place] += weighted(values, block)
        return carry

    lax.fori_loop(0, 2, step, 0)


def add_far(source, picks, z, norm, far_ref, place):
    p_ref, top = source
    rows = mm(pick_matrix(picks, PTS), p_ref[pl.ds(pl.multiple_of(top, 16), PTS), :]).astype(BF16)
    block = kern(rows, z, norm)
    w = p_ref[pl.ds(pl.multiple_of(top + PTS + 4 * RHS, 16), RHS), :]
    values = jnp.concatenate([w[:, :RANK], w[:, RANK:]], 0)
    far_ref[place] += weighted(values, block)


def load(source, target, semaphore):
    copy = pltpu.make_async_copy(source, target, semaphore)
    copy.start()
    copy.wait()


def self_body(flag_ref, z_ref, nz_ref, nx_ref, col_ref, both, near_ref, far_ref, own, semaphore):
    @pl.when(flag_ref[CORE] == 0)
    def _():
        load(both, own, semaphore)
        near_ref[...] = jnp.zeros_like(near_ref)
        far_ref[...] = jnp.zeros_like(far_ref)

        def leaf_terms(i, carry):
            x = own[pl.ds(pl.multiple_of(i * ROWS, 16), PTS), :]
            norm = nx_ref[i, 0:1, :]
            add_near((own, i * ROWS), x, norm, near_ref, i)
            other = (own, (1 - i) * ROWS)

            @pl.when(flag_ref[KIND + 8 * i] == 1)
            def _():
                add_near(other, x, norm, near_ref, i)

            @pl.when(flag_ref[KIND + 8 * i] == 2)
            def _():
                picks = jnp.where(i == 0, col_ref[:, 9:10], col_ref[:, 8:9])
                add_far(other, picks, z_ref[i], nz_ref[i, 0:1, :], far_ref, i)

            return carry

        lax.fori_loop(0, 2, leaf_terms, 0)


def group_body(first, flag_ref, z_ref, nz_ref, nx_ref, col_ref, near_in, far_in, both, *refs):
    arrivals = refs[:2]
    near_ref, far_ref, own, other, semaphore = refs[2:]

    def terms(slot):
        def pair_terms(n, carry):
            i, k = n >> 1, n & 1
            source = (other, k * ROWS)
            kind = flag_ref[KIND + 8 * i + slot + k]

            @pl.when(kind == 1)
            def _():
                x = own[pl.ds(pl.multiple_of(i * ROWS, 16), PTS), :]
                add_near(source, x, nx_ref[i, 0:1, :], near_ref, i)

            @pl.when(kind == 2)
            def _():
                picks = jnp.where(k == 0, col_ref[:, 9 + slot : 10 + slot], col_ref[:, 10 + slot : 11 + slot])
                add_far(source, picks, z_ref[i], nz_ref[i, 0:1, :], far_ref, i)

            return carry

        lax.fori_loop(0, 4, pair_terms, 0)

    @pl.when(flag_ref[CORE] == 0)
    def _():
        near_ref[...] = near_in[...]
        far_ref[...] = far_in[...]
        load(both, own, semaphore)
        if first:
            for k, slot in enumerate((1, 3)):

                @pl.when(flag_ref[KIND + slot] > 0)
                def _():
                    load(arrivals[k], other, semaphore)
                    terms(slot)
        else:
            for k in range(2):

                @pl.when(flag_ref[BEYOND] == 1 - k)
                def _():
                    load(arrivals[k], other, semaphore)

            terms(5)


def proxy_body(flag_ref, col_ref, right1, left1, right2, left2, out_ref, ends, other, near_ref, far_ref, z_ref, semaphore):
    @pl.when((flag_ref[CORE] == 0) & (flag_ref[SIDE] > 0))
    def _():
        near_ref[...] = jnp.zeros_like(near_ref)
        far_ref[...] = jnp.zeros_like(far_ref)

        @pl.when(flag_ref[SIDE] == 1)
        def _():
            load(right1, ends, semaphore)
            load(left2, other, semaphore)

        @pl.when(flag_ref[SIDE] == 2)
        def _():
            load(left1, ends, semaphore)
            load(right2, other, semaphore)

        def pair_terms(n, carry):
            i, k = n >> 1, n & 1
            source = (other, k * ROWS)
            kind = flag_ref[FARKIND + n]
            x = ends[pl.ds(pl.multiple_of(i * ROWS, 16), PTS), :]

            @pl.when(kind == 1)
            def _():
                add_near(source, x, row_norms(x)[0:1, :], near_ref, i)

            @pl.when(kind == 2)
            def _():
                picks = jnp.where(i == 0, col_ref[:, 16:17], col_ref[:, 17:18])
                z_ref[...] = mm(pick_matrix(picks, PTS), x).astype(BF16)
                z_norm = row_norms(z_ref[...])[0:1, :]
                far_picks = jnp.where(k == 0, col_ref[:, 14:15], col_ref[:, 15:16])
                add_far(source, far_picks, z_ref[...], z_norm, far_ref, i)

            return carry

        lax.fori_loop(0, 4, pair_terms, 0)

        out_ref[:, :, 0:PTS] = near_ref[...]
        out_ref[:, :, PTS:] = far_ref[...]


def node_body(height, last, flag_ref, col_ref, own_ref, sib_ref, *outs):
    outs = list(outs)

    @pl.when(flag_ref[CORE] == 1)
    def _():
        rest = list(outs)
        own = own_ref[...]
        sib = sib_ref[...]
        if not last:
            upper = flag_ref[BITS + height] * RANK
            picks = col_ref[:, height + 1 : height + 2]
            rows = mm(pick_matrix(picks - upper, RANK), own) + mm(pick_matrix(picks - (RANK - upper), RANK), sib)
            rest.pop(0)[...] = rows.astype(BF16)
        if height >= 3:
            rest.pop(0)[...] = kern(sib, own, row_norms(own)[0:1, :])


def mask_body(count, flag_ref, t_ref, w_ref, out_ref):
    for k in range(count):
        out_ref[k * RANK : (k + 1) * RANK, :] = pack(jnp.where(flag_ref[OWNED + k] == 1, t_ref[k + 1], 0.0))
    out_ref[count * RANK :, :] = pack(product(w_ref[...], t_ref[0]))


def sides(flag_ref, bit, size):
    upper = flag_ref[BITS + bit]
    return (
        pl.multiple_of(upper * size, 16),
        pl.multiple_of((1 - upper) * size, 16),
    )


def first_body(count, flag_ref, held_ref, arrived_ref, one_ref, two_ref, keep_ref, send_ref, lifted_ref):
    @pl.when(flag_ref[CORE] == 1)
    def _():
        one_ref[...] = held_ref[0:RANK, :] + arrived_ref[0:RANK, :]
        two = held_ref[RANK : 2 * RANK, :] + arrived_ref[RANK : 2 * RANK, :]
        two_ref[...] = two
        send_ref[0:RANK, :] = two
        keep, send = sides(flag_ref, 1, 128)
        for k in range(count - 2):
            mine = pl.ds((k + 2) * RANK + keep, 128)
            theirs = pl.ds((k + 2) * RANK + send, 128)
            keep_ref[k] = held_ref[mine, :] + arrived_ref[mine, :]
            send_ref[RANK + k * 128 : RANK + (k + 1) * 128, :] = held_ref[theirs, :] + arrived_ref[theirs, :]
        w = unpack(held_ref[count * RANK :, :]) + unpack(arrived_ref[count * RANK :, :])
        lifted = lift(w, one_ref[...])
        lifted_ref[...] = lifted
        send_ref[RANK + (count - 2) * 128 :, :] = pack(lifted)


def second_body(count, flag_ref, two_ref, held_ref, lifted_ref, arrived_ref, full_ref, keep_ref, send_ref, out_ref):
    @pl.when(flag_ref[CORE] == 1)
    def _():
        full_ref[...] = two_ref[...] + arrived_ref[0:RANK, :]
        keep, send = sides(flag_ref, 2, 64)
        for k in range(count - 2):
            top = RANK + k * 128
            keep_ref[k] = held_ref[k, pl.ds(keep, 64), :] + arrived_ref[pl.ds(top + keep, 64), :]
            send_ref[k * 64 : (k + 1) * 64, :] = held_ref[k, pl.ds(send, 64), :] + arrived_ref[pl.ds(top + send, 64), :]
        w = lifted_ref[...] + unpack(arrived_ref[RANK + (count - 2) * 128 :, :])
        lifted = lift(w, full_ref[...])
        out_ref[...] = lifted
        send_ref[(count - 2) * 64 :, :] = pack(lifted)


def third_body(count, held_ref, lifted_ref, arrived_ref, done_ref, rest_ref, w_ref):
    done_ref[...] = held_ref[0] + arrived_ref[0:64, :]
    for k in range(1, count - 2):
        rest_ref[k - 1] = held_ref[k] + arrived_ref[k * 64 : (k + 1) * 64, :]
    w_ref[...] = lifted_ref[...] + unpack(arrived_ref[(count - 2) * 64 :, :])


def add_body(held_ref, arrived_ref, done_ref, rest_ref):
    total = held_ref[...] + arrived_ref[...]
    done_ref[...] = total[0]
    rest_ref[...] = total[1:]


def gather_body(*refs):
    held_ref, arrived_ref, out_ref = refs[-3:]
    for k, ref in enumerate(refs[:-3]):
        out_ref[k] = ref[...]
    out_ref[len(refs) - 3] = held_ref[0] + arrived_ref[0]


def join_body(bit, flag_ref, held_ref, arrived_ref, *refs):
    lifting = len(refs) > 1
    out_ref = refs[-2] if lifting else refs[-1]

    @pl.when(flag_ref[CORE] == 1)
    def _():
        size = arrived_ref.shape[1]
        mine, theirs = sides(flag_ref, bit, size)
        for k in range(arrived_ref.shape[0]):
            out_ref[k, pl.ds(mine, size), :] = held_ref[k]
            out_ref[k, pl.ds(theirs, size), :] = arrived_ref[k]
        if lifting:
            w = refs[0][...]
            refs[-1][0:RHS, :] = lift(w, out_ref[0])
            refs[-1][RHS:, :] = w


def climb_body(place, lifted_ref, arrived_ref, pair_ref, out_ref):
    w = lifted_ref[0:RHS, :] + arrived_ref[0:RHS, :]
    out_ref[RHS:, :] = w
    out_ref[0:RHS, :] = lift(w, pair_ref[place])


def descend_body(levels, flag_ref, one_ref, two_ref, pairs_ref, *refs):
    out_ref = refs[-1]
    blocks = refs[0 : levels - 3]
    coeffs = refs[levels - 3 : -1]

    @pl.when(flag_ref[CORE] == 1)
    def _():
        def coupling(height):
            values = coeffs[height - 3]
            values = values[RHS:, :] if values.shape[0] > RHS else values[...]
            return product(values, blocks[height - 3][...])

        field = coupling(levels - 1)
        for height in range(levels - 2, 0, -1):
            matrix = one_ref[...] if height == 1 else two_ref[...] if height == 2 else pairs_ref[height - 3]
            field = lower(field, matrix)
            if height >= 3:
                field = field + coupling(height)
        out_ref[...] = field


def final_body(flag_ref, near_ref, far_ref, handed_ref, even_ref, odd_ref, v_ref, t_ref, held_ref, arrived_ref, out_ref):
    def finish(near, far, parent):
        field = product(parent, t_ref[0], NT) + far + even_ref[:, PTS:] + odd_ref[:, PTS:]
        out_ref[...] = near + even_ref[:, 0:PTS] + odd_ref[:, 0:PTS] + product(field, v_ref[...], NT)

    upper = flag_ref[CORE] == 1
    finish(
        jnp.where(upper, handed_ref[:, 0:PTS], near_ref[0]),
        jnp.where(upper, handed_ref[:, PTS:], far_ref[0]),
        jnp.where(upper, held_ref[...], arrived_ref[...]),
    )


def whole(points, weights, leaf_basis, transfer, skeleton_index, node_owner, near_list):
    count = lax.axis_size("leaf")
    levels = count.bit_length() - 1
    upper = levels - 2
    leaf = lax.axis_index("leaf")
    bits = [leaf >> b & 1 for b in range(levels)]
    core = bits[0]
    line = leaf >> 1 & 3
    start = leaf - leaf % GROUP
    everyone = range(count)

    def move(value, pairs):
        return lax.ppermute(value, "leaf", pairs)

    def cross(value, bit):
        return move(value, [(s, s ^ (1 << bit)) for s in everyone if s & 1])

    def shift(value, step, lines):
        return move(value, [(s, s + 2 * step) for s in everyone if s & 1 == 0 and (s >> 1 & 3) in lines])

    payload, w = call(
        prepare_body,
        [((ROWS, DIM), BF16), ((RHS, RANK), F32)],
        [points, weights.T, leaf_basis],
        flops=10**9,
    )
    partner = move(payload, [(s, s ^ 1) for s in everyone])
    both = jnp.concatenate([payload, partner], 0)
    right1 = shift(both, 1, (0, 1, 2))
    left1 = shift(both, -1, (1, 2, 3))
    right2 = shift(right1, 1, (1, 2))
    left2 = shift(left1, -1, (1, 2))

    beyond = line >= 2
    far_end = jnp.where(beyond, line - 2, line + 2)
    places = jnp.stack([line - 1, line - 1, line + 1, line + 1, far_end, far_end])
    cores = jnp.arange(6, dtype=jnp.int32) & 1
    there = (places >= 0) & (places <= 3)
    targets = jnp.where(there, places, 0) * 2 + cores
    end = start + jnp.where(line == 2, 3, 0) * 2
    works = (line == 1) | (line == 2)
    base = leaf - core
    rows = near_list.reshape(count // 2, 6)
    mine = lax.dynamic_slice(rows, (leaf >> 1, 0), (1, 6)).reshape(2, 3)
    ends_rows = lax.dynamic_slice(rows, (end >> 1, 0), (1, 6)).reshape(2, 3)

    def kinds_of(lists, first, spots, valid):
        position = (first % GROUP) + jnp.arange(2, dtype=jnp.int32)
        offsets = spots ^ position[:, None]
        listed = jnp.any(lists[:, None, :] == offsets[:, :, None], axis=2)
        return jnp.where(valid, jnp.where(listed, 1, 2), 0).astype(jnp.int32)

    other = (base % GROUP) + 1 - jnp.arange(2, dtype=jnp.int32)
    spots = jnp.concatenate([other[:, None], jnp.broadcast_to(targets, (2, 6))], 1)
    valid = jnp.concatenate([jnp.ones((1,), bool), there])
    kinds = jnp.pad(kinds_of(mine, base, spots, valid[None, :]), ((0, 0), (0, 1))).reshape(-1)
    far_kinds = kinds_of(ends_rows, end, jnp.broadcast_to(targets[4:6], (2, 2)), works).reshape(-1)
    side = jnp.where(line == 1, 1, jnp.where(line == 2, 2, 0))
    steps = jnp.arange(8, dtype=jnp.int32)
    bit_row = (leaf >> steps) & 1
    owners = jnp.pad(node_owner, ((0, 6 - node_owner.shape[0]), (0, 0))).reshape(-1)
    heights6 = jnp.arange(1, 7, dtype=jnp.int32)
    owner = jnp.take(owners, (heights6 - 1) * node_owner.shape[1] + (leaf >> heights6))
    owned = (owner == (leaf & ((1 << heights6) - 1))).astype(jnp.int32)
    flags = jnp.concatenate(
        [bit_row, owned, jnp.zeros((2,), jnp.int32), kinds, side[None], far_kinds,
         jnp.zeros((BEYOND - FARKIND - 4,), jnp.int32), beyond[None]]
    ).astype(jnp.int32)
    heights = jnp.minimum(steps, levels - 1)
    path = jnp.concatenate(
        [heights * skeleton_index.shape[1] + (leaf >> heights), leaf[None], leaf[None] ^ 1, start + targets,
         end[None], end[None] + 1]
    )
    cols = jnp.take(skeleton_index.reshape(-1, RANK), path, axis=0).T

    matrices = transfer[0]
    extra = upper - 2
    held = call(
        lambda *r: mask_body(upper, *r), [((upper * RANK + RHS, DIM), BF16)], [flags, matrices, w], smem=1,
    )[0]
    arrived = move(held, [(s, s + 1) for s in everyone if s & 1 == 0])
    one, two, keep, send, lifted = call(
        lambda *r: first_body(upper, *r),
        [((RANK, DIM), BF16), ((RANK, DIM), BF16), ((extra, 128, DIM), BF16),
         ((RANK + extra * 128 + RHS, DIM), BF16), ((RHS, RANK), F32)],
        [flags, held, arrived], smem=1,
    )
    two, keep, send, lifted = call(
        lambda *r: second_body(upper, *r),
        [((RANK, DIM), BF16), ((extra, 64, DIM), BF16), ((extra * 64 + RHS, DIM), BF16), ((RHS, RANK), F32)],
        [flags, two, keep, lifted, cross(send, 1)], smem=1,
    )
    done, keep, w3 = call(
        lambda *r: third_body(upper, *r),
        [((64, DIM), BF16), ((extra - 1, 64, DIM), BF16), ((RHS, RANK), F32)],
        [keep, lifted, cross(send, 2)],
    )
    quarters = [done]
    for bit in range(3, levels - 2):
        arrived = cross(keep, bit)
        if keep.shape[0] > 1:
            done, keep = call(
                add_body, [((64, DIM), BF16), ((keep.shape[0] - 1, 64, DIM), BF16)], [keep, arrived],
            )
            quarters.append(done)
    halves = call(gather_body, [((extra, 64, DIM), BF16)], quarters + [keep, arrived])[0]
    halves = call(
        lambda *r: join_body(2, *r), [((extra, 128, DIM), BF16)], [flags, halves, cross(halves, 2)], smem=1,
    )[0]
    pairs, lifted = call(
        lambda *r: join_body(1, *r), [((extra, RANK, DIM), BF16), ((2 * RHS, RANK), F32)],
        [flags, halves, cross(halves, 1), w3], smem=1,
    )

    z, norm_z, norm_x, rows = call(
        skeleton_body,
        [((2, RANK, DIM), BF16), ((2, 8, RANK), F32), ((2, 8, PTS), F32), ((RANK, DIM), BF16)],
        [flags, both, cols], smem=1,
    )
    blocks = []
    for height in range(1, levels):
        last = height + 1 == levels
        outs = ([] if last else [((RANK, DIM), BF16)]) + ([((RANK, RANK), F32)] if height >= 3 else [])
        result = call(
            lambda *refs: node_body(height, last, *refs),
            outs,
            [flags, cols, rows, cross(rows, height)],
            smem=1,
        )
        if height >= 3:
            blocks.append(result[-1])
        rows = result[0]

    coeffs = []
    for height in range(3, levels - 1):
        if height > 3:
            lifted = call(
                lambda *r: climb_body(height - 3, *r), [((2 * RHS, RANK), F32)], [lifted, arrived, pairs],
            )[0]
        arrived = cross(lifted, height)
        coeffs.append(arrived)
    top = lifted[:RHS] + arrived[:RHS]
    coeffs.append(cross(top, levels - 1))
    parent = call(
        lambda *refs: descend_body(levels, *refs), [((RHS, RANK), F32)],
        [flags, one, two, pairs] + blocks + coeffs, smem=1,
    )[0]
    parent_other = move(parent, [(s, s - 1) for s in everyone if s & 1])

    sums = [((2, RHS, PTS), F32), ((2, RHS, RANK), F32)]
    shared = [flags, z, norm_z, norm_x, cols]
    hold = pltpu.VMEM((2 * ROWS, DIM), BF16)
    near, far = call(
        self_body, sums, shared + [both], smem=1, far=1, scratch=[hold, pltpu.SemaphoreType.DMA], flops=5 * 10**9,
    )
    near, far = call(
        lambda *r: group_body(True, *r), sums, shared + [near, far, both, right1, left1],
        smem=1, far=3, scratch=[hold, hold, pltpu.SemaphoreType.DMA], flops=10**10,
    )
    proxy = call(
        proxy_body, [((2, RHS, PTS + RANK), F32)], [flags, cols, right1, left1, right2, left2],
        smem=1, far=4,
        scratch=[hold, hold, pltpu.VMEM((2, RHS, PTS), F32), pltpu.VMEM((2, RHS, RANK), F32),
                 pltpu.VMEM((RANK, DIM), BF16), pltpu.SemaphoreType.DMA],
        flops=5 * 10**9,
    )[0]
    workers = [s for s in everyone if s & 1 == 0 and (s >> 1 & 3) in (1, 2)]
    step = lambda s: 2 if (s >> 1 & 3) == 2 else -2
    even = move(proxy[0], [(s, s + step(s)) for s in workers])
    odd = move(proxy[1], [(s, s + step(s) + 1) for s in workers])
    near, far = call(
        lambda *r: group_body(False, *r), sums, shared + [near, far, both, right2, left2],
        smem=1, far=3, scratch=[hold, hold, pltpu.SemaphoreType.DMA], flops=5 * 10**9,
    )
    handed = move(jnp.concatenate([near[1], far[1]], 1), [(s, s + 1) for s in everyone if s & 1 == 0])
    out = call(
        final_body, [((RHS, PTS), F32)],
        [flags, near, far, handed, even, odd, leaf_basis, matrices[0:1], parent, parent_other], smem=1, flops=10**9,
    )[0]
    return out.T


def solution(mesh):
    return jax.shard_map(
        whole,
        mesh=mesh,
        in_specs=(
            P("leaf", None),
            P("leaf", None),
            P("leaf", None),
            P("leaf", None, None, None),
            P(),
            P(),
            P(),
        ),
        out_specs=P("leaf", None),
        check_vma=False,
    )
```

profile of v0, /device:TPU:1, one launch (start us, length us, event | category | flops | bytes accessed | tf_op | source)
XLA Modules:
  0.0 215.8 jit_solution(5634773125127950918)
XLA Ops:
  3.9 3.3 %collective-permute-start = (bf16[1344,512]{1,0:T(8,128)(2,1)S(1)}, bf16[1344,512]{1,0:T(8,128)(2,1)}, u32[]{:S(2)}, u32[]{:S(2)}) collective-permute-start(bf16[1344,512]{1,0:T(8,128)(2,1)S(1)} %get-tuple-element.43), channel_id=1, source_target_pairs={{0,1},{1,0},{2,3},{3,2},{4,5},{5,4},{6,7},{7,6},{8,9},{9,8},{10,11... | collective-permute-start | bytes 4128776 | tf_op jit(solution)/shard_map/ppermute | solution.py:441
  36.5 4.1 %collective-permute-done.8.r_2_ = bf16[1600,512]{1,0:T(8,128)(2,1)S(1)} collective-permute-done((bf16[1600,512]{1,0:T(8,128)(2,1)S(1)}, bf16[1600,512]{1,0:T(8,128)(2,1)S(1)}, u32[]{:S(2)}, u32[]{:S(2)}) %collective-permute-start.8) | collective-permute-done | bytes 1638432 | tf_op jit(solution)/shard_map/ppermute | solution.py:441
  44.5 3.7 %collective-permute-start.9 = (bf16[832,512]{1,0:T(8,128)(2,1)}, bf16[832,512]{1,0:T(8,128)(2,1)S(1)}, u32[]{:S(2)}, u32[]{:S(2)}) collective-permute-start(bf16[832,512]{1,0:T(8,128)(2,1)} %get-tuple-element.58), channel_id=1, source_target_pairs={{1,3},{3,1},{5,7},{7,5},{9,11},{11,9},{13,15},{15,13},{17,19},{19,... | collective-permute-start | bytes 2555912 | tf_op jit(solution)/shard_map/ppermute | solution.py:441
  48.5 19.6 %collective-permute-done.9.r_4_ = bf16[832,512]{1,0:T(8,128)(2,1)S(1)} collective-permute-done((bf16[832,512]{1,0:T(8,128)(2,1)}, bf16[832,512]{1,0:T(8,128)(2,1)S(1)}, u32[]{:S(2)}, u32[]{:S(2)}) %collective-permute-start.9) | collective-permute-done | bytes 852000 | tf_op jit(solution)/shard_map/ppermute | solution.py:441
  72.8 4.9 %collective-permute-start.10 = (bf16[320,512]{1,0:T(8,128)(2,1)}, bf16[320,512]{1,0:T(8,128)(2,1)S(1)}, u32[]{:S(2)}, u32[]{:S(2)}) collective-permute-start(bf16[320,512]{1,0:T(8,128)(2,1)} %get-tuple-element.62), channel_id=1, source_target_pairs={{1,5},{3,7},{5,1},{7,3},{9,13},{11,15},{13,9},{15,11},{17,21},{19,... | collective-permute-start | bytes 983048 | tf_op jit(solution)/shard_map/ppermute | solution.py:441
  81.5 6.5 %collective-permute-done.10.r_2_ = bf16[320,512]{1,0:T(8,128)(2,1)S(1)} collective-permute-done((bf16[320,512]{1,0:T(8,128)(2,1)}, bf16[320,512]{1,0:T(8,128)(2,1)S(1)}, u32[]{:S(2)}, u32[]{:S(2)}) %collective-permute-start.10) | collective-permute-done | bytes 327712 | tf_op jit(solution)/shard_map/ppermute | solution.py:441
  89.1 7.3 %collective-permute-start.11 = (bf16[3,64,512]{2,1,0:T(8,128)(2,1)S(1)}, bf16[3,64,512]{2,1,0:T(8,128)(2,1)S(1)}, u32[]{:S(2)}, u32[]{:S(2)}) collective-permute-start(bf16[3,64,512]{2,1,0:T(8,128)(2,1)S(1)} %get-tuple-element.64.held_ref), channel_id=1, source_target_pairs={{1,9},{3,11},{5,13},{7,15},{9,1},{11,3},{13,5},{15,7},{17,25},{19,... | collective-permute-start | bytes 589832 | tf_op jit(solution)/shard_map/ppermute | solution.py:441
  96.3 4.4 %shard_map.74 = (bf16[2,256,512]{2,1,0:T(8,128)(2,1)S(1)}, f32[2,8,256]{2,1,0:T(8,128)S(1)}, f32[2,8,1024]{2,1,0:T(8,128)S(1)}, bf16[256,512]{1,0:T(8,128)(2,1)S(1)}) custom-call(s32[41]{0:T(128)S(1)} %concatenate.78.flag_ref.r_0_.refs_0_, bf16[2688,512]{1,0:T(8,128)(2,1)} %constant_dynamic-update-slice_fusion.both_ref.both.r_7_, ...), custom_call_target="tpu_custom_call" | custom-call | bytes 2771108 | tf_op jit(solution)/shard_map/pallas_call | solution.py:82
  103.8 3.1 %collective-permute-start.12 = (bf16[2,64,512]{2,1,0:T(8,128)(2,1)S(1)}, bf16[2,64,512]{2,1,0:T(8,128)(2,1)S(1)}, u32[]{:S(2)}, u32[]{:S(2)}) collective-permute-start(bf16[2,64,512]{2,1,0:T(8,128)(2,1)S(1)} %get-tuple-element.66.held_ref), channel_id=1, source_target_pairs={{1,17},{3,19},{5,21},{7,23},{9,25},{11,27},{13,29},{15,31},{17,1},... | collective-permute-start | bytes 393224 | tf_op jit(solution)/shard_map/ppermute | solution.py:441
  106.9 4.2 %collective-permute-done.16.refs_3_ = bf16[256,512]{1,0:T(8,128)(2,1)S(1)} collective-permute-done((bf16[256,512]{1,0:T(8,128)(2,1)S(1)}, bf16[256,512]{1,0:T(8,128)(2,1)S(1)}, u32[]{:S(2)}, u32[]{:S(2)}) %collective-permute-start.16) | collective-permute-done | bytes 262176 | tf_op jit(solution)/shard_map/ppermute | solution.py:441
  112.0 3.4 %collective-permute-start.17 = (bf16[256,512]{1,0:T(8,128)(2,1)S(1)}, bf16[256,512]{1,0:T(8,128)(2,1)S(1)}, u32[]{:S(2)}, u32[]{:S(2)}) collective-permute-start(bf16[256,512]{1,0:T(8,128)(2,1)S(1)} %shard_map.88.refs_2_), channel_id=1, source_target_pairs={{1,5},{3,7},{5,1},{7,3},{9,13},{11,15},{13,9},{15,11},{17,21},{19,... | collective-permute-start | bytes 786440 | tf_op jit(solution)/shard_map/ppermute | solution.py:441
  115.4 4.6 %collective-permute-start.13 = (bf16[1,64,512]{2,1,0:T(8,128)(2,1)S(1)}, bf16[1,64,512]{2,1,0:T(8,128)(2,1)S(1)}, u32[]{:S(2)}, u32[]{:S(2)}) collective-permute-start(bf16[1,64,512]{2,1,0:T(8,128)(2,1)S(1)} %get-tuple-element.68.refs_3_), channel_id=1, source_target_pairs={{1,33},{3,35},{5,37},{7,39},{9,41},{11,43},{13,45},{15,47},{17,49}... | collective-permute-start | bytes 196616 | tf_op jit(solution)/shard_map/ppermute | solution.py:441
  126.1 3.2 %collective-permute-start.18 = (bf16[256,512]{1,0:T(8,128)(2,1)S(1)}, bf16[256,512]{1,0:T(8,128)(2,1)S(1)}, u32[]{:S(2)}, u32[]{:S(2)}) collective-permute-start(bf16[256,512]{1,0:T(8,128)(2,1)S(1)} %shard_map.89.refs_2_), channel_id=1, source_target_pairs={{1,9},{3,11},{5,13},{7,15},{9,1},{11,3},{13,5},{15,7},{17,25},{19,... | collective-permute-start | bytes 786440 | tf_op jit(solution)/shard_map/ppermute | solution.py:441
  129.2 3.6 %collective-permute-done.14.r_2_ = bf16[4,64,512]{2,1,0:T(8,128)(2,1)S(1)} collective-permute-done((bf16[4,64,512]{2,1,0:T(8,128)(2,1)S(1)}, bf16[4,64,512]{2,1,0:T(8,128)(2,1)S(1)}, u32[]{:S(2)}, u32[]{:S(2)}) %collective-permute-start.14) | collective-permute-done | bytes 262176 | tf_op jit(solution)/shard_map/ppermute | solution.py:441
  133.5 5.0 %collective-permute-start.15 = (bf16[4,128,512]{2,1,0:T(8,128)(2,1)S(1)}, bf16[4,128,512]{2,1,0:T(8,128)(2,1)S(1)}, u32[]{:S(2)}, u32[]{:S(2)}) collective-permute-start(bf16[4,128,512]{2,1,0:T(8,128)(2,1)S(1)} %shard_map.86.r_1_), channel_id=1, source_target_pairs={{1,3},{3,1},{5,7},{7,5},{9,11},{11,9},{13,15},{15,13},{17,19},{19,... | collective-permute-start | bytes 1572872 | tf_op jit(solution)/shard_map/ppermute | solution.py:441
  139.7 3.1 %collective-permute-start.19 = (bf16[256,512]{1,0:T(8,128)(2,1)S(1)}, bf16[256,512]{1,0:T(8,128)(2,1)S(1)}, u32[]{:S(2)}, u32[]{:S(2)}) collective-permute-start(bf16[256,512]{1,0:T(8,128)(2,1)S(1)} %get-tuple-element.73.refs_2_), channel_id=1, source_target_pairs={{1,17},{3,19},{5,21},{7,23},{9,25},{11,27},{13,29},{15,31},{17,1},... | collective-permute-start | bytes 786440 | tf_op jit(solution)/shard_map/ppermute | solution.py:441
  142.8 4.0 %collective-permute-done.19.refs_3_ = bf16[256,512]{1,0:T(8,128)(2,1)S(1)} collective-permute-done((bf16[256,512]{1,0:T(8,128)(2,1)S(1)}, bf16[256,512]{1,0:T(8,128)(2,1)S(1)}, u32[]{:S(2)}, u32[]{:S(2)}) %collective-permute-start.19) | collective-permute-done | bytes 262176 | tf_op jit(solution)/shard_map/ppermute | solution.py:441
  147.9 4.7 %collective-permute-start.20 = (bf16[256,512]{1,0:T(8,128)(2,1)S(1)}, bf16[256,512]{1,0:T(8,128)(2,1)S(1)}, u32[]{:S(2)}, u32[]{:S(2)}) collective-permute-start(bf16[256,512]{1,0:T(8,128)(2,1)S(1)} %get-tuple-element.75.refs_2_), channel_id=1, source_target_pairs={{1,33},{3,35},{5,37},{7,39},{9,41},{11,43},{13,45},{15,47},{17,49}... | collective-permute-start | bytes 786440 | tf_op jit(solution)/shard_map/ppermute | solution.py:441
  157.7 3.2 %collective-permute-start.21 = (bf16[256,512]{1,0:T(8,128)(2,1)S(1)}, bf16[256,512]{1,0:T(8,128)(2,1)S(1)}, u32[]{:S(2)}, u32[]{:S(2)}) collective-permute-start(bf16[256,512]{1,0:T(8,128)(2,1)S(1)} %get-tuple-element.77.refs_2_), channel_id=1, source_target_pairs={{1,65},{3,67},{5,69},{7,71},{9,73},{11,75},{13,77},{15,79},{17,81}... | collective-permute-start | bytes 786440 | tf_op jit(solution)/shard_map/ppermute | solution.py:441
  167.4 4.8 %collective-permute-start.22 = (bf16[256,512]{1,0:T(8,128)(2,1)S(1)}, bf16[256,512]{1,0:T(8,128)(2,1)S(1)}, u32[]{:S(2)}, u32[]{:S(2)}) collective-permute-start(bf16[256,512]{1,0:T(8,128)(2,1)S(1)} %get-tuple-element.79.refs_2_), channel_id=1, source_target_pairs={{1,129},{3,131},{5,133},{7,135},{9,137},{11,139},{13,141},{15,143}... | collective-permute-start | bytes 786440 | tf_op jit(solution)/shard_map/ppermute | solution.py:441
  172.5 3.6 %collective-permute-start.25 = (f32[128,256]{1,0:T(8,128)S(1)}, f32[128,256]{1,0:T(8,128)S(1)}, u32[]{:S(2)}, u32[]{:S(2)}) collective-permute-start(f32[128,256]{1,0:T(8,128)S(1)} %shard_map.96.r_0_), channel_id=1, source_target_pairs={{1,33},{3,35},{5,37},{7,39},{9,41},{11,43},{13,45},{15,47},{17,49}... | collective-permute-start | bytes 393224 | tf_op jit(solution)/shard_map/ppermute | solution.py:441
  176.7 3.0 %collective-permute-done.25.r_1_.refs_11_ = f32[128,256]{1,0:T(8,128)S(1)} collective-permute-done((f32[128,256]{1,0:T(8,128)S(1)}, f32[128,256]{1,0:T(8,128)S(1)}, u32[]{:S(2)}, u32[]{:S(2)}) %collective-permute-start.25) | collective-permute-done | bytes 131104 | tf_op jit(solution)/shard_map/ppermute | solution.py:441
  187.1 3.5 %collective-permute-start.27 = (f32[64,256]{1,0:T(8,128)S(1)}, f32[64,256]{1,0:T(8,128)S(1)}, u32[]{:S(2)}, u32[]{:S(2)}) collective-permute-start(f32[64,256]{1,0:T(8,128)S(1)} %slice_add_fusion), channel_id=1, source_target_pairs={{1,129},{3,131},{5,133},{7,135},{9,137},{11,139},{13,141},{15,143}... | collective-permute-start | bytes 196616 | tf_op jit(solution)/shard_map/ppermute | solution.py:441
  198.1 15.7 %collective-permute-done.7.odd_ref = f32[64,1280]{1,0:T(8,128)S(1)} collective-permute-done((f32[64,1280]{1,0:T(8,128)S(1)}, f32[64,1280]{1,0:T(8,128)S(1)}, u32[]{:S(2)}, u32[]{:S(2)}) %collective-permute-start.7) | collective-permute-done | bytes 327712 | tf_op jit(solution)/shard_map/ppermute | solution.py:441
  (145 shorter events, 88.5 us)
Async XLA Ops:
  3.9 21.9 %collective-permute-start = (bf16[1344,512]{1,0:T(8,128)(2,1)S(1)}, bf16[1344,512]{1,0:T(8,128)(2,1)}, u32[]{:S(2)}, u32[]{:S(2)}) collective-permute-start(bf16[1344,512]{1,0:T(8,128)(2,1)S(1)} %get-tuple-element.43), channel_id=1, source_target_pairs={{0,1},{1,0},{2,3},{3,2},{4,5},{5,4},{6,7},{7,6},{8,9},{9,8},{10,11... | collective-permute-start | bytes 4128776 | tf_op jit(solution)/shard_map/ppermute | solution.py:441
  28.3 50.1 %collective-permute-start.1 = (bf16[2688,512]{1,0:T(8,128)(2,1)}, bf16[2688,512]{1,0:T(8,128)(2,1)}, u32[]{:S(2)}, u32[]{:S(2)}) collective-permute-start(bf16[2688,512]{1,0:T(8,128)(2,1)} %constant_dynamic-update-slice_fusion.both_ref.both.r_7_), channel_id=1, source_target_pairs={{0,2},{2,4},{4,6},{8,10},{10,12},{12,14},{16,18},{18,20},{20,22},{... | collective-permute-start | bytes 8257544 | tf_op jit(solution)/shard_map/ppermute | solution.py:441
  30.4 48.8 %collective-permute-start.2 = (bf16[2688,512]{1,0:T(8,128)(2,1)}, bf16[2688,512]{1,0:T(8,128)(2,1)}, u32[]{:S(2)}, u32[]{:S(2)}) collective-permute-start(bf16[2688,512]{1,0:T(8,128)(2,1)} %constant_dynamic-update-slice_fusion.both_ref.both.r_7_), channel_id=1, source_target_pairs={{2,0},{4,2},{6,4},{10,8},{12,10},{14,12},{18,16},{20,18},{22,20},{... | collective-permute-start | bytes 8257544 | tf_op jit(solution)/shard_map/ppermute | solution.py:441
  44.5 23.5 %collective-permute-start.9 = (bf16[832,512]{1,0:T(8,128)(2,1)}, bf16[832,512]{1,0:T(8,128)(2,1)S(1)}, u32[]{:S(2)}, u32[]{:S(2)}) collective-permute-start(bf16[832,512]{1,0:T(8,128)(2,1)} %get-tuple-element.58), channel_id=1, source_target_pairs={{1,3},{3,1},{5,7},{7,5},{9,11},{11,9},{13,15},{15,13},{17,19},{19,... | collective-permute-start | bytes 2555912 | tf_op jit(solution)/shard_map/ppermute | solution.py:441
  72.8 15.3 %collective-permute-start.10 = (bf16[320,512]{1,0:T(8,128)(2,1)}, bf16[320,512]{1,0:T(8,128)(2,1)S(1)}, u32[]{:S(2)}, u32[]{:S(2)}) collective-permute-start(bf16[320,512]{1,0:T(8,128)(2,1)} %get-tuple-element.62), channel_id=1, source_target_pairs={{1,5},{3,7},{5,1},{7,3},{9,13},{11,15},{13,9},{15,11},{17,21},{19,... | collective-permute-start | bytes 983048 | tf_op jit(solution)/shard_map/ppermute | solution.py:441
  78.4 103.8 %collective-permute-start.3 = (bf16[2688,512]{1,0:T(8,128)(2,1)}, bf16[2688,512]{1,0:T(8,128)(2,1)S(1)}, u32[]{:S(2)}, u32[]{:S(2)}) collective-permute-start(bf16[2688,512]{1,0:T(8,128)(2,1)} %collective-permute-done.1.r_8_.right1), channel_id=1, source_target_pairs={{2,4},{4,6},{10,12},{12,14},{18,20},{20,22},{26,28},{28,30},{34,36... | collective-permute-start | bytes 8257544 | tf_op jit(solution)/shard_map/ppermute | solution.py:441
  79.2 103.0 %collective-permute-start.4 = (bf16[2688,512]{1,0:T(8,128)(2,1)}, bf16[2688,512]{1,0:T(8,128)(2,1)}, u32[]{:S(2)}, u32[]{:S(2)}) collective-permute-start(bf16[2688,512]{1,0:T(8,128)(2,1)} %collective-permute-done.2.r_9_.left1), channel_id=1, source_target_pairs={{2,0},{4,2},{10,8},{12,10},{18,16},{20,18},{26,24},{28,26},{34,32}... | collective-permute-start | bytes 8257544 | tf_op jit(solution)/shard_map/ppermute | solution.py:441
  89.1 14.7 %collective-permute-start.11 = (bf16[3,64,512]{2,1,0:T(8,128)(2,1)S(1)}, bf16[3,64,512]{2,1,0:T(8,128)(2,1)S(1)}, u32[]{:S(2)}, u32[]{:S(2)}) collective-permute-start(bf16[3,64,512]{2,1,0:T(8,128)(2,1)S(1)} %get-tuple-element.64.held_ref), channel_id=1, source_target_pairs={{1,9},{3,11},{5,13},{7,15},{9,1},{11,3},{13,5},{15,7},{17,25},{19,... | collective-permute-start | bytes 589832 | tf_op jit(solution)/shard_map/ppermute | solution.py:441
  100.8 10.3 %collective-permute-start.16 = (bf16[256,512]{1,0:T(8,128)(2,1)S(1)}, bf16[256,512]{1,0:T(8,128)(2,1)S(1)}, u32[]{:S(2)}, u32[]{:S(2)}) collective-permute-start(bf16[256,512]{1,0:T(8,128)(2,1)S(1)} %get-tuple-element.71.refs_2_), channel_id=1, source_target_pairs={{1,3},{3,1},{5,7},{7,5},{9,11},{11,9},{13,15},{15,13},{17,19},{19,... | collective-permute-start | bytes 786440 | tf_op jit(solution)/shard_map/ppermute | solution.py:441
  103.8 11.6 %collective-permute-start.12 = (bf16[2,64,512]{2,1,0:T(8,128)(2,1)S(1)}, bf16[2,64,512]{2,1,0:T(8,128)(2,1)S(1)}, u32[]{:S(2)}, u32[]{:S(2)}) collective-permute-start(bf16[2,64,512]{2,1,0:T(8,128)(2,1)S(1)} %get-tuple-element.66.held_ref), channel_id=1, source_target_pairs={{1,17},{3,19},{5,21},{7,23},{9,25},{11,27},{13,29},{15,31},{17,1},... | collective-permute-start | bytes 393224 | tf_op jit(solution)/shard_map/ppermute | solution.py:441
  112.0 13.1 %collective-permute-start.17 = (bf16[256,512]{1,0:T(8,128)(2,1)S(1)}, bf16[256,512]{1,0:T(8,128)(2,1)S(1)}, u32[]{:S(2)}, u32[]{:S(2)}) collective-permute-start(bf16[256,512]{1,0:T(8,128)(2,1)S(1)} %shard_map.88.refs_2_), channel_id=1, source_target_pairs={{1,5},{3,7},{5,1},{7,3},{9,13},{11,15},{13,9},{15,11},{17,21},{19,... | collective-permute-start | bytes 786440 | tf_op jit(solution)/shard_map/ppermute | solution.py:441
  122.0 10.9 %collective-permute-start.14 = (bf16[4,64,512]{2,1,0:T(8,128)(2,1)S(1)}, bf16[4,64,512]{2,1,0:T(8,128)(2,1)S(1)}, u32[]{:S(2)}, u32[]{:S(2)}) collective-permute-start(bf16[4,64,512]{2,1,0:T(8,128)(2,1)S(1)} %shard_map.85.r_1_), channel_id=1, source_target_pairs={{1,5},{3,7},{5,1},{7,3},{9,13},{11,15},{13,9},{15,11},{17,21},{19,... | collective-permute-start | bytes 786440 | tf_op jit(solution)/shard_map/ppermute | solution.py:441
  126.1 12.5 %collective-permute-start.18 = (bf16[256,512]{1,0:T(8,128)(2,1)S(1)}, bf16[256,512]{1,0:T(8,128)(2,1)S(1)}, u32[]{:S(2)}, u32[]{:S(2)}) collective-permute-start(bf16[256,512]{1,0:T(8,128)(2,1)S(1)} %shard_map.89.refs_2_), channel_id=1, source_target_pairs={{1,9},{3,11},{5,13},{7,15},{9,1},{11,3},{13,5},{15,7},{17,25},{19,... | collective-permute-start | bytes 786440 | tf_op jit(solution)/shard_map/ppermute | solution.py:441
  133.5 19.1 %collective-permute-start.15 = (bf16[4,128,512]{2,1,0:T(8,128)(2,1)S(1)}, bf16[4,128,512]{2,1,0:T(8,128)(2,1)S(1)}, u32[]{:S(2)}, u32[]{:S(2)}) collective-permute-start(bf16[4,128,512]{2,1,0:T(8,128)(2,1)S(1)} %shard_map.86.r_1_), channel_id=1, source_target_pairs={{1,3},{3,1},{5,7},{7,5},{9,11},{11,9},{13,15},{15,13},{17,19},{19,... | collective-permute-start | bytes 1572872 | tf_op jit(solution)/shard_map/ppermute | solution.py:441
  147.9 8.6 %collective-permute-start.20 = (bf16[256,512]{1,0:T(8,128)(2,1)S(1)}, bf16[256,512]{1,0:T(8,128)(2,1)S(1)}, u32[]{:S(2)}, u32[]{:S(2)}) collective-permute-start(bf16[256,512]{1,0:T(8,128)(2,1)S(1)} %get-tuple-element.75.refs_2_), channel_id=1, source_target_pairs={{1,33},{3,35},{5,37},{7,39},{9,41},{11,43},{13,45},{15,47},{17,49}... | collective-permute-start | bytes 786440 | tf_op jit(solution)/shard_map/ppermute | solution.py:441
  153.4 9.7 %collective-permute-start.23 = (f32[128,256]{1,0:T(8,128)S(1)}, f32[128,256]{1,0:T(8,128)S(1)}, u32[]{:S(2)}, u32[]{:S(2)}) collective-permute-start(f32[128,256]{1,0:T(8,128)S(1)} %get-tuple-element.80.r_0_), channel_id=1, source_target_pairs={{1,9},{3,11},{5,13},{7,15},{9,1},{11,3},{13,5},{15,7},{17,25},{19,... | collective-permute-start | bytes 393224 | tf_op jit(solution)/shard_map/ppermute | solution.py:441
  157.7 8.6 %collective-permute-start.21 = (bf16[256,512]{1,0:T(8,128)(2,1)S(1)}, bf16[256,512]{1,0:T(8,128)(2,1)S(1)}, u32[]{:S(2)}, u32[]{:S(2)}) collective-permute-start(bf16[256,512]{1,0:T(8,128)(2,1)S(1)} %get-tuple-element.77.refs_2_), channel_id=1, source_target_pairs={{1,65},{3,67},{5,69},{7,71},{9,73},{11,75},{13,77},{15,79},{17,81}... | collective-permute-start | bytes 786440 | tf_op jit(solution)/shard_map/ppermute | solution.py:441
  163.3 9.0 %collective-permute-start.24 = (f32[128,256]{1,0:T(8,128)S(1)}, f32[128,256]{1,0:T(8,128)S(1)}, u32[]{:S(2)}, u32[]{:S(2)}) collective-permute-start(f32[128,256]{1,0:T(8,128)S(1)} %shard_map.95.r_0_), channel_id=1, source_target_pairs={{1,17},{3,19},{5,21},{7,23},{9,25},{11,27},{13,29},{15,31},{17,1},... | collective-permute-start | bytes 393224 | tf_op jit(solution)/shard_map/ppermute | solution.py:441
  167.4 23.1 %collective-permute-start.22 = (bf16[256,512]{1,0:T(8,128)(2,1)S(1)}, bf16[256,512]{1,0:T(8,128)(2,1)S(1)}, u32[]{:S(2)}, u32[]{:S(2)}) collective-permute-start(bf16[256,512]{1,0:T(8,128)(2,1)S(1)} %get-tuple-element.79.refs_2_), channel_id=1, source_target_pairs={{1,129},{3,131},{5,133},{7,135},{9,137},{11,139},{13,141},{15,143}... | collective-permute-start | bytes 786440 | tf_op jit(solution)/shard_map/ppermute | solution.py:441
  172.5 7.2 %collective-permute-start.25 = (f32[128,256]{1,0:T(8,128)S(1)}, f32[128,256]{1,0:T(8,128)S(1)}, u32[]{:S(2)}, u32[]{:S(2)}) collective-permute-start(f32[128,256]{1,0:T(8,128)S(1)} %shard_map.96.r_0_), channel_id=1, source_target_pairs={{1,33},{3,35},{5,37},{7,39},{9,41},{11,43},{13,45},{15,47},{17,49}... | collective-permute-start | bytes 393224 | tf_op jit(solution)/shard_map/ppermute | solution.py:441
  179.9 7.2 %collective-permute-start.26 = (f32[128,256]{1,0:T(8,128)S(1)}, f32[128,256]{1,0:T(8,128)S(1)}, u32[]{:S(2)}, u32[]{:S(2)}) collective-permute-start(f32[128,256]{1,0:T(8,128)S(1)} %shard_map.97), channel_id=1, source_target_pairs={{1,65},{3,67},{5,69},{7,71},{9,73},{11,75},{13,77},{15,79},{17,81}... | collective-permute-start | bytes 393224 | tf_op jit(solution)/shard_map/ppermute | solution.py:441
  182.9 15.2 %collective-permute-start.5 = (f32[64,1280]{1,0:T(8,128)S(1)}, f32[64,1280]{1,0:T(8,128)S(1)}, u32[]{:S(2)}, u32[]{:S(2)}) collective-permute-start(f32[64,1280]{1,0:T(8,128)S(1)} %pad_maximum_fusion), channel_id=1, source_target_pairs={{0,1},{2,3},{4,5},{6,7},{8,9},{10,11},{12,13},{14,15},{16,17},{18,... | collective-permute-start | bytes 983048 | tf_op jit(solution)/shard_map/ppermute | solution.py:441
  185.0 13.1 %collective-permute-start.6 = (f32[64,1280]{1,0:T(8,128)S(1)}, f32[64,1280]{1,0:T(8,128)S(1)}, u32[]{:S(2)}, u32[]{:S(2)}) collective-permute-start(f32[64,1280]{1,0:T(8,128)S(1)} %get-tuple-element.86), channel_id=1, source_target_pairs={{2,0},{4,6},{10,8},{12,14},{18,16},{20,22},{26,24},{28,30},{34,32}... | collective-permute-start | bytes 983048 | tf_op jit(solution)/shard_map/ppermute | solution.py:441
  185.8 28.1 %collective-permute-start.7 = (f32[64,1280]{1,0:T(8,128)S(1)}, f32[64,1280]{1,0:T(8,128)S(1)}, u32[]{:S(2)}, u32[]{:S(2)}) collective-permute-start(f32[64,1280]{1,0:T(8,128)S(1)} %get-tuple-element.85), channel_id=1, source_target_pairs={{2,1},{4,7},{10,9},{12,15},{18,17},{20,23},{26,25},{28,31},{34,33}... | collective-permute-start | bytes 983048 | tf_op jit(solution)/shard_map/ppermute | solution.py:441
  (22 other events, 175.2 us)
where the time goes:
time: 217 us; the launch traced here: 216 us
  starting transfers between devices  87.5 us (40%)
  waiting for transfers between devices  68.3 us (31%)
  local copies, waits for them, and re-layouts  27.2 us (13%)
  Pallas kernels  24.8 us (11%)
  other arithmetic  7.35 us (3%)
    ppermute x29, starting transfers between devices, move(): return lax.ppermute(value, 'leaf', pairs)  87.5 us
    ppermute x29, waiting for transfers between devices, move(): return lax.ppermute(value, 'leaf', pairs)  68.3 us
    pallas_call x27, Pallas kernels, call(): pl.pallas_call(body, out_shape=[jax.ShapeDtypeStruct(s, d) for s, d in ou...  24.8 us
    unnamed x36, local copies, waits for them, and re-layouts  13.9 us
  transfers between devices with their start and end apart: 29, of which 13 were waited for; matrix products, arithmetic and copies ran while one was open for 10% of the time, Pallas kernels for 10%

commit v1 on v0

v1 whole, which is shorter than its diff:
```python
import jax
import jax.numpy as jnp
from jax import lax
from jax.experimental import pallas as pl
from jax.experimental.pallas import tpu as pltpu
from jax.sharding import PartitionSpec as P


GROUP = 8
PTS = 1024
DIM = 512
RANK = 256
RHS = 64
ROWS = PTS + 4 * RHS + RHS
SCALE = 2.0 / DIM
INTERPRET = False

F32 = jnp.float32
BF16 = jnp.bfloat16
NN = (((1,), (0,)), ((), ()))
NT = (((1,), (1,)), ((), ()))


def mm(a, b, dims=NN):
    return lax.dot_general(a, b, dims, preferred_element_type=F32)


def split(a):
    high = a.astype(BF16)
    return high, (a - high.astype(F32)).astype(BF16)


def product(a, b, dims=NN):
    a_high, a_low = split(a)
    b_high, b_low = split(b)
    rows = a.shape[0]
    both = mm(jnp.concatenate([a_high, a_low], 0), b_high, dims)
    return both[:rows] + both[rows:] + mm(a_high, b_low, dims)


def row_norms(rows):
    wide = rows.astype(F32)
    high, low = split(wide * wide)
    ones = jnp.ones((8, rows.shape[1]), BF16)
    return mm(ones, high, NT) + mm(ones, low, NT)


def kern(left, right, right_norm):
    wide = left.astype(F32)
    left_norm = jnp.sum(wide * wide, axis=1, keepdims=True)
    inner = mm(left, right, NT)
    return jnp.exp(-SCALE * (left_norm + right_norm - 2.0 * inner))


def pick_matrix(picks, count):
    lanes = lax.broadcasted_iota(jnp.int32, (picks.shape[0], count), 1)
    return jnp.where(lanes == picks, 1.0, 0.0).astype(BF16)


def weighted(values, block):
    half = values.shape[0] // 2
    high, low = split(block)
    both = mm(values, high)
    return both[:half] + both[half:] + mm(values[:half], low)


def call(body, outs, args, smem=0, flops=0, far=0, scratch=(), hbm=False):
    near = len(args) - far
    in_specs = [
        pl.BlockSpec(memory_space=pltpu.SMEM if k < smem else pltpu.VMEM if k < near else pltpu.HBM)
        for k in range(len(args))
    ]
    size = sum(a.size * a.dtype.itemsize for a in args)
    return pl.pallas_call(
        body,
        out_shape=[jax.ShapeDtypeStruct(s, d) for s, d in outs],
        in_specs=in_specs,
        out_specs=[pl.BlockSpec(memory_space=pltpu.HBM if hbm else pltpu.VMEM) for _ in outs],
        scratch_shapes=list(scratch),
        compiler_params=pltpu.CompilerParams(vmem_limit_bytes=40 << 20),
        cost_estimate=pl.CostEstimate(flops=flops, transcendentals=0, bytes_accessed=size),
        interpret=INTERPRET,
    )(*args)


def lift(values, pair):
    high, low = split(values)
    rows = values.shape[0]
    both = mm(jnp.concatenate([high, low], 0), pair[:, :RANK])
    return both[:rows] + both[rows:] + mm(high, pair[:, RANK:])


def lower(values, pair):
    high, low = split(values)
    rows = values.shape[0]
    both = mm(jnp.concatenate([high, low], 0), pair[:, :RANK], NT)
    return both[:rows] + both[rows:] + mm(high, pair[:, RANK:], NT)


def pack(values):
    high, low = split(values)
    return jnp.concatenate([high, low], 1)


def unpack(pair):
    return pair[:, :RANK].astype(F32) + pair[:, RANK:].astype(F32)


def prepare_body(x_ref, b_ref, v_ref, p_ref, w_ref):
    b_high, b_low = split(b_ref[...])
    v_high, v_low = split(v_ref[...])
    both = mm(jnp.concatenate([b_high, b_low], 0), v_high)
    w = both[:RHS] + both[RHS:] + mm(b_high, v_low)
    w_ref[...] = w
    p_ref[0:PTS, :] = x_ref[...]
    for k, part in enumerate((b_high[:, :DIM], b_low[:, :DIM], b_high[:, DIM:], b_low[:, DIM:])):
        p_ref[PTS + k * RHS : PTS + (k + 1) * RHS, :] = part
    p_ref[PTS + 4 * RHS :, :] = pack(w)


def bit_of(leaf_ref, bit):
    return leaf_ref[0] >> bit & 1


def column(col_ref, lane):
    lanes = lax.broadcasted_iota(jnp.int32, col_ref.shape, 1)
    picked = jnp.where(lanes == lane, col_ref[...].astype(F32), 0.0)
    return jnp.sum(picked, axis=1, keepdims=True).astype(jnp.int32)


def kind_of(near_ref, leaf, other):
    offset = leaf ^ other
    listed = (near_ref[0, leaf] == offset) | (near_ref[1, leaf] == offset) | (near_ref[2, leaf] == offset)
    return jnp.where(listed, 1, 2)


def skeleton_body(x_ref, col_ref, z_ref):
    z_ref[...] = mm(pick_matrix(col_ref[:, 0:1], PTS), x_ref[...]).astype(BF16)


def add_near(source, x, norm, near_ref, place):
    p_ref, top = source

    def step(k, carry):
        for h in range(2):
            first = pl.multiple_of(top + k * 512 + h * 256, 16)
            block = kern(p_ref[pl.ds(first, 256), :], x, norm)
            row = pl.multiple_of(top + PTS + k * (2 * RHS), 16)
            values = p_ref[pl.ds(row, 2 * RHS), h * 256 : (h + 1) * 256]
            near_ref[place] += weighted(values, block)
        return carry

    lax.fori_loop(0, 2, step, 0)


def add_far(source, picks, z, norm, far_ref, place):
    p_ref, top = source
    rows = mm(pick_matrix(picks, PTS), p_ref[pl.ds(pl.multiple_of(top, 16), PTS), :]).astype(BF16)
    block = kern(rows, z, norm)
    w = p_ref[pl.ds(pl.multiple_of(top + PTS + 4 * RHS, 16), RHS), :]
    values = jnp.concatenate([w[:, :RANK], w[:, RANK:]], 0)
    far_ref[place] += weighted(values, block)


def load(source, target, semaphore):
    copy = pltpu.make_async_copy(source, target, semaphore)
    copy.start()
    copy.wait()


def stack_body(leaf_ref, first, second, out, semaphore):
    @pl.when(bit_of(leaf_ref, 0) == 0)
    def _():
        load(first, out.at[pl.ds(0, ROWS), :], semaphore)
        load(second, out.at[pl.ds(ROWS, ROWS), :], semaphore)


def self_body(leaf_ref, near_list, col_ref, both, near_ref, far_ref, z_ref, nz_ref, nx_ref, own, semaphore):
    leaf = leaf_ref[0]

    @pl.when(leaf & 1 == 0)
    def _():
        load(both, own, semaphore)
        near_ref[...] = jnp.zeros_like(near_ref)
        far_ref[...] = jnp.zeros_like(far_ref)

        def leaf_terms(i, carry):
            x = own[pl.ds(pl.multiple_of(i * ROWS, 16), PTS), :]
            norm = row_norms(x)
            z = mm(pick_matrix(column(col_ref, 8 + ((leaf + i) & 7)), PTS), x).astype(BF16)
            z_norm = row_norms(z)
            nx_ref[i] = norm
            z_ref[i] = z
            nz_ref[i] = z_norm
            add_near((own, i * ROWS), x, norm[0:1, :], near_ref, i)
            source = (own, (1 - i) * ROWS)
            other = leaf + 1 - i
            kind = kind_of(near_list, leaf + i, other)

            @pl.when(kind == 1)
            def _():
                add_near(source, x, norm[0:1, :], near_ref, i)

            @pl.when(kind == 2)
            def _():
                add_far(source, column(col_ref, 8 + (other & 7)), z, z_norm[0:1, :], far_ref, i)

            return carry

        lax.fori_loop(0, 2, leaf_terms, 0)


def group_body(first, leaf_ref, near_list, col_ref, z_ref, nz_ref, nx_ref, near_in, far_in, both, *refs):
    arrivals = refs[:2]
    near_ref, far_ref, own, arrived, semaphore = refs[2:]
    leaf = leaf_ref[0]
    line = leaf >> 1 & 3

    def terms(place):
        def pair_terms(n, carry):
            i, k = n >> 1, n & 1
            source = (arrived, k * ROWS)
            other = leaf - (leaf & 7) + 2 * place + k
            kind = kind_of(near_list, leaf + i, other)

            @pl.when(kind == 1)
            def _():
                x = own[pl.ds(pl.multiple_of(i * ROWS, 16), PTS), :]
                add_near(source, x, nx_ref[i, 0:1, :], near_ref, i)

            @pl.when(kind == 2)
            def _():
                add_far(source, column(col_ref, 8 + (other & 7)), z_ref[i], nz_ref[i, 0:1, :], far_ref, i)

            return carry

        lax.fori_loop(0, 4, pair_terms, 0)

    @pl.when(leaf & 1 == 0)
    def _():
        near_ref[...] = near_in[...]
        far_ref[...] = far_in[...]
        load(both, own, semaphore)
        if first:

            @pl.when(line > 0)
            def _():
                load(arrivals[0], arrived, semaphore)
                terms(line - 1)

            @pl.when(line < 3)
            def _():
                load(arrivals[1], arrived, semaphore)
                terms(line + 1)
        else:

            @pl.when(line >= 2)
            def _():
                load(arrivals[0], arrived, semaphore)

            @pl.when(line < 2)
            def _():
                load(arrivals[1], arrived, semaphore)

            terms(jnp.where(line >= 2, line - 2, line + 2))


def proxy_body(leaf_ref, near_list, col_ref, right1, left1, right2, left2,
               out_ref, ends, arrived, near_ref, far_ref, z_ref, semaphore):
    leaf = leaf_ref[0]
    line = leaf >> 1 & 3
    start = leaf - (leaf & 7)

    @pl.when((leaf & 1 == 0) & ((line == 1) | (line == 2)))
    def _():
        near_ref[...] = jnp.zeros_like(near_ref)
        far_ref[...] = jnp.zeros_like(far_ref)

        @pl.when(line == 1)
        def _():
            load(right1, ends, semaphore)
            load(left2, arrived, semaphore)

        @pl.when(line == 2)
        def _():
            load(left1, ends, semaphore)
            load(right2, arrived, semaphore)

        client = start + jnp.where(line == 1, 0, 6)
        distant = start + jnp.where(line == 1, 6, 0)

        def pair_terms(n, carry):
            i, k = n >> 1, n & 1
            source = (arrived, k * ROWS)
            kind = kind_of(near_list, client + i, distant + k)
            x = ends[pl.ds(pl.multiple_of(i * ROWS, 16), PTS), :]

            @pl.when(kind == 1)
            def _():
                add_near(source, x, row_norms(x)[0:1, :], near_ref, i)

            @pl.when(kind == 2)
            def _():
                z_ref[...] = mm(pick_matrix(column(col_ref, 8 + ((client + i) & 7)), PTS), x).astype(BF16)
                z_norm = row_norms(z_ref[...])[0:1, :]
                add_far(source, column(col_ref, 8 + ((distant + k) & 7)), z_ref[...], z_norm, far_ref, i)

            return carry

        lax.fori_loop(0, 4, pair_terms, 0)
        out_ref[:, :, 0:PTS] = near_ref[...]
        out_ref[:, :, PTS:] = far_ref[...]


def node_body(height, last, flag_ref, col_ref, own_ref, sib_ref, *outs):
    outs = list(outs)

    @pl.when(bit_of(flag_ref, 0) == 1)
    def _():
        rest = list(outs)
        own = own_ref[...]
        sib = sib_ref[...]
        if not last:
            upper = bit_of(flag_ref, height) * RANK
            picks = col_ref[:, height + 1 : height + 2]
            rows = mm(pick_matrix(picks - upper, RANK), own) + mm(pick_matrix(picks - (RANK - upper), RANK), sib)
            rest.pop(0)[...] = rows.astype(BF16)
        if height >= 3:
            rest.pop(0)[...] = kern(sib, own, row_norms(own)[0:1, :])


def mask_body(count, leaf_ref, owner_ref, t_ref, w_ref, out_ref, leaf_pair_ref):
    leaf = leaf_ref[0]
    for k in range(count):
        mine = owner_ref[k, leaf >> (k + 1)] == leaf & ((2 << k) - 1)
        out_ref[k * RANK : (k + 1) * RANK, :] = pack(jnp.where(mine, t_ref[k + 1], 0.0))
    pair = pack(t_ref[0])
    leaf_pair_ref[...] = pair
    out_ref[count * RANK :, :] = pack(lift(w_ref[...], pair))


def sides(flag_ref, bit, size):
    upper = bit_of(flag_ref, bit)
    return (
        pl.multiple_of(upper * size, 16),
        pl.multiple_of((1 - upper) * size, 16),
    )


def first_body(count, flag_ref, held_ref, arrived_ref, one_ref, two_ref, keep_ref, send_ref, lifted_ref):
    @pl.when(bit_of(flag_ref, 0) == 1)
    def _():
        one_ref[...] = held_ref[0:RANK, :] + arrived_ref[0:RANK, :]
        two = held_ref[RANK : 2 * RANK, :] + arrived_ref[RANK : 2 * RANK, :]
        two_ref[...] = two
        send_ref[0:RANK, :] = two
        keep, send = sides(flag_ref, 1, 128)
        for k in range(count - 2):
            mine = pl.ds((k + 2) * RANK + keep, 128)
            theirs = pl.ds((k + 2) * RANK + send, 128)
            keep_ref[k] = held_ref[mine, :] + arrived_ref[mine, :]
            send_ref[RANK + k * 128 : RANK + (k + 1) * 128, :] = held_ref[theirs, :] + arrived_ref[theirs, :]
        w = unpack(held_ref[count * RANK :, :]) + unpack(arrived_ref[count * RANK :, :])
        lifted = lift(w, one_ref[...])
        lifted_ref[...] = lifted
        send_ref[RANK + (count - 2) * 128 :, :] = pack(lifted)


def second_body(count, flag_ref, two_ref, held_ref, lifted_ref, arrived_ref, full_ref, keep_ref, send_ref, out_ref):
    @pl.when(bit_of(flag_ref, 0) == 1)
    def _():
        full_ref[...] = two_ref[...] + arrived_ref[0:RANK, :]
        keep, send = sides(flag_ref, 2, 64)
        for k in range(count - 2):
            top = RANK + k * 128
            keep_ref[k] = held_ref[k, pl.ds(keep, 64), :] + arrived_ref[pl.ds(top + keep, 64), :]
            send_ref[k * 64 : (k + 1) * 64, :] = held_ref[k, pl.ds(send, 64), :] + arrived_ref[pl.ds(top + send, 64), :]
        w = lifted_ref[...] + unpack(arrived_ref[RANK + (count - 2) * 128 :, :])
        lifted = lift(w, full_ref[...])
        out_ref[...] = lifted
        send_ref[(count - 2) * 64 :, :] = pack(lifted)


def third_body(count, held_ref, lifted_ref, arrived_ref, done_ref, rest_ref, w_ref):
    done_ref[...] = held_ref[0] + arrived_ref[0:64, :]
    for k in range(1, count - 2):
        rest_ref[k - 1] = held_ref[k] + arrived_ref[k * 64 : (k + 1) * 64, :]
    w_ref[...] = lifted_ref[...] + unpack(arrived_ref[(count - 2) * 64 :, :])


def add_body(held_ref, arrived_ref, done_ref, rest_ref):
    total = held_ref[...] + arrived_ref[...]
    done_ref[...] = total[0]
    rest_ref[...] = total[1:]


def gather_body(*refs):
    held_ref, arrived_ref, out_ref = refs[-3:]
    for k, ref in enumerate(refs[:-3]):
        out_ref[k] = ref[...]
    out_ref[len(refs) - 3] = held_ref[0] + arrived_ref[0]


def join_body(bit, flag_ref, held_ref, arrived_ref, *refs):
    lifting = len(refs) > 1
    out_ref = refs[-2] if lifting else refs[-1]

    @pl.when(bit_of(flag_ref, 0) == 1)
    def _():
        size = arrived_ref.shape[1]
        mine, theirs = sides(flag_ref, bit, size)
        for k in range(arrived_ref.shape[0]):
            out_ref[k, pl.ds(mine, size), :] = held_ref[k]
            out_ref[k, pl.ds(theirs, size), :] = arrived_ref[k]
        if lifting:
            w = refs[0][...]
            refs[-1][0:RHS, :] = lift(w, out_ref[0])
            refs[-1][RHS:, :] = w


def climb_body(place, lifted_ref, arrived_ref, pair_ref, out_ref):
    w = lifted_ref[0:RHS, :] + arrived_ref[0:RHS, :]
    out_ref[RHS:, :] = w
    out_ref[0:RHS, :] = lift(w, pair_ref[place])


def descend_body(levels, flag_ref, one_ref, two_ref, pairs_ref, *refs):
    out_ref = refs[-1]
    blocks = refs[0 : levels - 3]
    coeffs = refs[levels - 3 : -1]

    @pl.when(bit_of(flag_ref, 0) == 1)
    def _():
        def coupling(height):
            values = coeffs[height - 3]
            values = values[RHS:, :] if values.shape[0] > RHS else values[...]
            return product(values, blocks[height - 3][...])

        field = coupling(levels - 1)
        for height in range(levels - 2, 0, -1):
            matrix = one_ref[...] if height == 1 else two_ref[...] if height == 2 else pairs_ref[height - 3]
            field = lower(field, matrix)
            if height >= 3:
                field = field + coupling(height)
        out_ref[...] = field


def final_body(flag_ref, near_ref, far_ref, handed_ref, even_ref, odd_ref, v_ref, t_ref, held_ref, arrived_ref, out_ref):
    def finish(near, far, parent):
        field = lower(parent, t_ref[...]) + far + even_ref[:, PTS:] + odd_ref[:, PTS:]
        out_ref[...] = near + even_ref[:, 0:PTS] + odd_ref[:, 0:PTS] + product(field, v_ref[...], NT)

    upper = bit_of(flag_ref, 0) == 1
    finish(
        jnp.where(upper, handed_ref[:, 0:PTS], near_ref[0]),
        jnp.where(upper, handed_ref[:, PTS:], far_ref[0]),
        jnp.where(upper, held_ref[...], arrived_ref[...]),
    )


def whole(points, weights, leaf_basis, transfer, skeleton_index, node_owner, near_list):
    count = lax.axis_size("leaf")
    levels = count.bit_length() - 1
    upper = levels - 2
    leaf = lax.axis_index("leaf")
    everyone = range(count)

    def move(value, pairs):
        return lax.ppermute(value, "leaf", pairs)

    def cross(value, bit):
        return move(value, [(s, s ^ (1 << bit)) for s in everyone if s & 1])

    def to_tree(value):
        return move(value, [(s, s + 1) for s in everyone if s & 1 == 0])

    def shift(value, step, lines):
        return move(value, [(s, s + 2 * step) for s in everyone if s & 1 == 0 and (s >> 1 & 3) in lines])

    place = leaf.astype(jnp.int32)[None]
    near_rows = near_list.T
    columns = jnp.arange(16, dtype=jnp.int32)
    heights = jnp.minimum(columns, levels - 1)
    path = jnp.where(
        columns < 8, heights * skeleton_index.shape[1] + (leaf >> heights), leaf - leaf % GROUP + columns - 8
    )
    cols = skeleton_index.reshape(-1, RANK).at[path].get(mode="promise_in_bounds").T

    payload, w = call(
        prepare_body,
        [((ROWS, DIM), BF16), ((RHS, RANK), F32)],
        [points, weights.T, leaf_basis],
        flops=10**9,
    )
    partner = move(payload, [(s, s ^ 1) for s in everyone])
    both = call(
        stack_body, [((2 * ROWS, DIM), BF16)], [place, payload, partner], smem=1, far=2,
        scratch=[pltpu.SemaphoreType.DMA], hbm=True,
    )[0]
    right1 = shift(both, 1, (0, 1, 2))
    left1 = shift(both, -1, (1, 2, 3))
    right2 = shift(right1, 1, (1, 2))
    left2 = shift(left1, -1, (1, 2))

    matrices = transfer[0]
    extra = upper - 2
    held, leaf_pair = call(
        lambda *r: mask_body(upper, *r), [((upper * RANK + RHS, DIM), BF16), ((RANK, DIM), BF16)],
        [place, node_owner, matrices, w], smem=2,
    )
    arrived = to_tree(held)
    one, two, keep, send, lifted = call(
        lambda *r: first_body(upper, *r),
        [((RANK, DIM), BF16), ((RANK, DIM), BF16), ((extra, 128, DIM), BF16),
         ((RANK + extra * 128 + RHS, DIM), BF16), ((RHS, RANK), F32)],
        [place, held, arrived], smem=1,
    )
    two, keep, send, lifted = call(
        lambda *r: second_body(upper, *r),
        [((RANK, DIM), BF16), ((extra, 64, DIM), BF16), ((extra * 64 + RHS, DIM), BF16), ((RHS, RANK), F32)],
        [place, two, keep, lifted, cross(send, 1)], smem=1,
    )
    done, keep, w3 = call(
        lambda *r: third_body(upper, *r),
        [((64, DIM), BF16), ((extra - 1, 64, DIM), BF16), ((RHS, RANK), F32)],
        [keep, lifted, cross(send, 2)],
    )
    quarters = [done]
    for bit in range(3, levels - 2):
        arrived = cross(keep, bit)
        if keep.shape[0] > 1:
            done, keep = call(
                add_body, [((64, DIM), BF16), ((keep.shape[0] - 1, 64, DIM), BF16)], [keep, arrived],
            )
            quarters.append(done)
    halves = call(gather_body, [((extra, 64, DIM), BF16)], quarters + [keep, arrived])[0]
    halves = call(
        lambda *r: join_body(2, *r), [((extra, 128, DIM), BF16)], [place, halves, cross(halves, 2)], smem=1,
    )[0]
    pairs, lifted = call(
        lambda *r: join_body(1, *r), [((extra, RANK, DIM), BF16), ((2 * RHS, RANK), F32)],
        [place, halves, cross(halves, 1), w3], smem=1,
    )

    rows = call(skeleton_body, [((RANK, DIM), BF16)], [points, cols])[0]
    blocks = []
    for height in range(levels):
        last = height + 1 == levels
        outs = ([] if last else [((RANK, DIM), BF16)]) + ([((RANK, RANK), F32)] if height >= 3 else [])
        result = call(
            lambda *refs: node_body(height, last, *refs),
            outs,
            [place, cols, rows, cross(rows, height) if height else to_tree(rows)],
            smem=1,
        )
        if height >= 3:
            blocks.append(result[-1])
        rows = result[0]

    coeffs = []
    for height in range(3, levels - 1):
        if height > 3:
            lifted = call(
                lambda *r: climb_body(height - 3, *r), [((2 * RHS, RANK), F32)], [lifted, arrived, pairs],
            )[0]
        arrived = cross(lifted, height)
        coeffs.append(arrived)
    top = lifted[:RHS] + arrived[:RHS]
    coeffs.append(cross(top, levels - 1))
    parent = call(
        lambda *refs: descend_body(levels, *refs), [((RHS, RANK), F32)],
        [place, one, two, pairs] + blocks + coeffs, smem=1,
    )[0]
    parent_other = move(parent, [(s, s - 1) for s in everyone if s & 1])

    sums = [((2, RHS, PTS), F32), ((2, RHS, RANK), F32)]
    shared = [place, near_rows, cols]
    hold = pltpu.VMEM((2 * ROWS, DIM), BF16)
    near, far, z, norm_z, norm_x = call(
        self_body, sums + [((2, RANK, DIM), BF16), ((2, 8, RANK), F32), ((2, 8, PTS), F32)], shared + [both],
        smem=2, far=1, scratch=[hold, pltpu.SemaphoreType.DMA], flops=5 * 10**9,
    )
    near, far = call(
        lambda *r: group_body(True, *r), sums, shared + [z, norm_z, norm_x, near, far, both, right1, left1],
        smem=2, far=3, scratch=[hold, hold, pltpu.SemaphoreType.DMA], flops=10**10,
    )
    proxy = call(
        proxy_body, [((2, RHS, PTS + RANK), F32)], shared + [right1, left1, right2, left2],
        smem=2, far=4,
        scratch=[hold, hold, pltpu.VMEM((2, RHS, PTS), F32), pltpu.VMEM((2, RHS, RANK), F32),
                 pltpu.VMEM((RANK, DIM), BF16), pltpu.SemaphoreType.DMA],
        flops=5 * 10**9,
    )[0]
    workers = [s for s in everyone if s & 1 == 0 and (s >> 1 & 3) in (1, 2)]
    step = lambda s: 2 if (s >> 1 & 3) == 2 else -2
    even = move(proxy[0], [(s, s + step(s)) for s in workers])
    odd = move(proxy[1], [(s, s + step(s) + 1) for s in workers])
    near, far = call(
        lambda *r: group_body(False, *r), sums, shared + [z, norm_z, norm_x, near, far, both, right2, left2],
        smem=2, far=3, scratch=[hold, hold, pltpu.SemaphoreType.DMA], flops=5 * 10**9,
    )
    handed = move(jnp.concatenate([near[1], far[1]], 1), [(s, s + 1) for s in everyone if s & 1 == 0])
    out = call(
        final_body, [((RHS, PTS), F32)],
        [place, near, far, handed, even, odd, leaf_basis, leaf_pair, parent, parent_other], smem=1, flops=10**9,
    )[0]
    return out.T


def solution(mesh):
    return jax.shard_map(
        whole,
        mesh=mesh,
        in_specs=(
            P("leaf", None),
            P("leaf", None),
            P("leaf", None),
            P("leaf", None, None, None),
            P(),
            P(),
            P(),
        ),
        out_specs=P("leaf", None),
        check_vma=False,
    )
```

time: 217 us -> 193 us (0.89)
  local copies, waits for them, and re-layouts: 27.2 us -> 12.9 us
  Pallas kernels: 24.8 us -> 16.8 us
  other arithmetic: 7.35 us -> 0.05 us
  starting transfers between devices: 87.5 us -> 92.1 us
    pallas_call x27 -> x29, Pallas kernels: 24.8 us -> 16.8 us  [call(): pl.pallas_call(body, out_shape=[jax.ShapeDtypeStruct(s, d) for s, d in ou...]
    ppermute x29 -> x30, starting transfers between devices: 87.5 us -> 92.1 us  [move(): return lax.ppermute(value, 'leaf', pairs)]
    concatenate x5 -> x0, local copies, waits for them, and re-layouts: 3.42 us -> none  [the longest x1 2.52 us: whole(): both = jnp.concatenate([payload, partner], 0)]
    eq x2 -> x0, local copies, waits for them, and re-layouts: 2.48 us -> none  [kinds_of(): listed = jnp.any(lists[:, None, :] == offsets[:, :, None], axis=2)]
    reshape x3 -> x0, local copies, waits for them, and re-layouts: 2.39 us -> none  [the longest x1 1.61 us: whole(): rows = near_list.reshape(count // 2, 6)]
    unnamed x36 -> x42, local copies, waits for them, and re-layouts: 13.9 us -> 12.1 us
    ppermute x29 -> x30, waiting for transfers between devices: 68.3 us -> 69.5 us  [move(): return lax.ppermute(value, 'leaf', pairs)]
  transfers between devices with their start and end apart: 29 -> 30, of which waited for: 13 -> 13; matrix products, arithmetic and copies ran while one was open for 10% -> 0% of each run, Pallas kernels for 10% -> 8%
where the time goes in v1:
time: 193 us; the launch traced here: 192 us
  starting transfers between devices  92.1 us (48%)
  waiting for transfers between devices  69.5 us (36%)
  Pallas kernels  16.8 us (9%)
  local copies, waits for them, and re-layouts  12.9 us (7%)
    ppermute x30, starting transfers between devices, move(): return lax.ppermute(value, 'leaf', pairs)  92.1 us
    ppermute x30, waiting for transfers between devices, move(): return lax.ppermute(value, 'leaf', pairs)  69.5 us
    pallas_call x29, Pallas kernels, call(): pl.pallas_call(body, out_shape=[jax.ShapeDtypeStruct(s, d) for s, d in ou...  16.8 us
    unnamed x42, local copies, waits for them, and re-layouts  12.1 us
  transfers between devices with their start and end apart: 30, of which 13 were waited for; matrix products, arithmetic and copies ran while one was open for 0% of the time, Pallas kernels for 8%

profile of v1, /device:TPU:1, one launch (start us, length us, event | category | flops | bytes accessed | tf_op | source)
XLA Modules:
  0.0 191.9 jit_solution(11145634556553751101)
XLA Ops:
  3.9 3.3 %collective-permute-start = (bf16[1344,512]{1,0:T(8,128)(2,1)S(1)}, bf16[1344,512]{1,0:T(8,128)(2,1)}, u32[]{:S(2)}, u32[]{:S(2)}) collective-permute-start(bf16[1344,512]{1,0:T(8,128)(2,1)S(1)} %get-tuple-element.44.first), channel_id=1, source_target_pairs={{0,1},{1,0},{2,3},{3,2},{4,5},{5,4},{6,7},{7,6},{8,9},{9,8},{10,11... | collective-permute-start | bytes 4128776 | tf_op jit(solution)/shard_map/ppermute | solution.py:469
  20.9 11.8 %collective-permute-done.9.r_4_ = bf16[832,512]{1,0:T(8,128)(2,1)} collective-permute-done((bf16[832,512]{1,0:T(8,128)(2,1)}, bf16[832,512]{1,0:T(8,128)(2,1)}, u32[]{:S(2)}, u32[]{:S(2)}) %collective-permute-start.9) | collective-permute-done | bytes 852000 | tf_op jit(solution)/shard_map/ppermute | solution.py:469
  38.0 3.4 %collective-permute-start.10 = (bf16[320,512]{1,0:T(8,128)(2,1)}, bf16[320,512]{1,0:T(8,128)(2,1)}, u32[]{:S(2)}, u32[]{:S(2)}) collective-permute-start(bf16[320,512]{1,0:T(8,128)(2,1)} %get-tuple-element.65), channel_id=1, source_target_pairs={{1,5},{3,7},{5,1},{7,3},{9,13},{11,15},{13,9},{15,11},{17,21},{19,... | collective-permute-start | bytes 983048 | tf_op jit(solution)/shard_map/ppermute | solution.py:469
  45.6 4.9 %collective-permute-done.10.r_2_ = bf16[320,512]{1,0:T(8,128)(2,1)} collective-permute-done((bf16[320,512]{1,0:T(8,128)(2,1)}, bf16[320,512]{1,0:T(8,128)(2,1)}, u32[]{:S(2)}, u32[]{:S(2)}) %collective-permute-start.10) | collective-permute-done | bytes 327712 | tf_op jit(solution)/shard_map/ppermute | solution.py:469
  53.3 7.1 %collective-permute-start.11 = (bf16[3,64,512]{2,1,0:T(8,128)(2,1)S(1)}, bf16[3,64,512]{2,1,0:T(8,128)(2,1)S(1)}, u32[]{:S(2)}, u32[]{:S(2)}) collective-permute-start(bf16[3,64,512]{2,1,0:T(8,128)(2,1)S(1)} %get-tuple-element.67.held_ref), channel_id=1, source_target_pairs={{1,9},{3,11},{5,13},{7,15},{9,1},{11,3},{13,5},{15,7},{17,25},{19,... | collective-permute-start | bytes 589832 | tf_op jit(solution)/shard_map/ppermute | solution.py:469
  60.4 15.4 %collective-permute-done.16.refs_3_ = bf16[256,512]{1,0:T(8,128)(2,1)S(1)} collective-permute-done((bf16[256,512]{1,0:T(8,128)(2,1)S(1)}, bf16[256,512]{1,0:T(8,128)(2,1)S(1)}, u32[]{:S(2)}, u32[]{:S(2)}) %collective-permute-start.16) | collective-permute-done | bytes 262176 | tf_op jit(solution)/shard_map/ppermute | solution.py:469
  76.1 4.3 %collective-permute-start.17 = (bf16[256,512]{1,0:T(8,128)(2,1)S(1)}, bf16[256,512]{1,0:T(8,128)(2,1)S(1)}, u32[]{:S(2)}, u32[]{:S(2)}) collective-permute-start(bf16[256,512]{1,0:T(8,128)(2,1)S(1)} %shard_map.89.refs_2_), channel_id=1, source_target_pairs={{1,3},{3,1},{5,7},{7,5},{9,11},{11,9},{13,15},{15,13},{17,19},{19,... | collective-permute-start | bytes 786440 | tf_op jit(solution)/shard_map/ppermute | solution.py:469
  80.5 3.1 %collective-permute-start.12 = (bf16[2,64,512]{2,1,0:T(8,128)(2,1)S(1)}, bf16[2,64,512]{2,1,0:T(8,128)(2,1)S(1)}, u32[]{:S(2)}, u32[]{:S(2)}) collective-permute-start(bf16[2,64,512]{2,1,0:T(8,128)(2,1)S(1)} %get-tuple-element.69.held_ref), channel_id=1, source_target_pairs={{1,17},{3,19},{5,21},{7,23},{9,25},{11,27},{13,29},{15,31},{17,1},... | collective-permute-start | bytes 393224 | tf_op jit(solution)/shard_map/ppermute | solution.py:469
  83.6 3.8 %collective-permute-done.17.refs_3_ = bf16[256,512]{1,0:T(8,128)(2,1)S(1)} collective-permute-done((bf16[256,512]{1,0:T(8,128)(2,1)S(1)}, bf16[256,512]{1,0:T(8,128)(2,1)S(1)}, u32[]{:S(2)}, u32[]{:S(2)}) %collective-permute-start.17) | collective-permute-done | bytes 262176 | tf_op jit(solution)/shard_map/ppermute | solution.py:469
  87.7 4.9 %collective-permute-start.18 = (bf16[256,512]{1,0:T(8,128)(2,1)S(1)}, bf16[256,512]{1,0:T(8,128)(2,1)S(1)}, u32[]{:S(2)}, u32[]{:S(2)}) collective-permute-start(bf16[256,512]{1,0:T(8,128)(2,1)S(1)} %shard_map.90.refs_2_), channel_id=1, source_target_pairs={{1,5},{3,7},{5,1},{7,3},{9,13},{11,15},{13,9},{15,11},{17,21},{19,... | collective-permute-start | bytes 786440 | tf_op jit(solution)/shard_map/ppermute | solution.py:469
  92.7 4.6 %collective-permute-start.13 = (bf16[1,64,512]{2,1,0:T(8,128)(2,1)S(1)}, bf16[1,64,512]{2,1,0:T(8,128)(2,1)S(1)}, u32[]{:S(2)}, u32[]{:S(2)}) collective-permute-start(bf16[1,64,512]{2,1,0:T(8,128)(2,1)S(1)} %get-tuple-element.71.refs_3_), channel_id=1, source_target_pairs={{1,33},{3,35},{5,37},{7,39},{9,41},{11,43},{13,45},{15,47},{17,49}... | collective-permute-start | bytes 196616 | tf_op jit(solution)/shard_map/ppermute | solution.py:469
  101.5 7.3 %collective-permute-start.19 = (bf16[256,512]{1,0:T(8,128)(2,1)S(1)}, bf16[256,512]{1,0:T(8,128)(2,1)S(1)}, u32[]{:S(2)}, u32[]{:S(2)}) collective-permute-start(bf16[256,512]{1,0:T(8,128)(2,1)S(1)} %shard_map.91.refs_2_), channel_id=1, source_target_pairs={{1,9},{3,11},{5,13},{7,15},{9,1},{11,3},{13,5},{15,7},{17,25},{19,... | collective-permute-start | bytes 786440 | tf_op jit(solution)/shard_map/ppermute | solution.py:469
  108.8 7.1 %collective-permute-done.14.r_2_ = bf16[4,64,512]{2,1,0:T(8,128)(2,1)S(1)} collective-permute-done((bf16[4,64,512]{2,1,0:T(8,128)(2,1)S(1)}, bf16[4,64,512]{2,1,0:T(8,128)(2,1)S(1)}, u32[]{:S(2)}, u32[]{:S(2)}) %collective-permute-start.14) | collective-permute-done | bytes 262176 | tf_op jit(solution)/shard_map/ppermute | solution.py:469
  118.6 3.1 %collective-permute-start.20 = (bf16[256,512]{1,0:T(8,128)(2,1)S(1)}, bf16[256,512]{1,0:T(8,128)(2,1)S(1)}, u32[]{:S(2)}, u32[]{:S(2)}) collective-permute-start(bf16[256,512]{1,0:T(8,128)(2,1)S(1)} %get-tuple-element.75.refs_2_), channel_id=1, source_target_pairs={{1,17},{3,19},{5,21},{7,23},{9,25},{11,27},{13,29},{15,31},{17,1},... | collective-permute-start | bytes 786440 | tf_op jit(solution)/shard_map/ppermute | solution.py:469
  121.7 4.3 %collective-permute-done.20.refs_3_ = bf16[256,512]{1,0:T(8,128)(2,1)S(1)} collective-permute-done((bf16[256,512]{1,0:T(8,128)(2,1)S(1)}, bf16[256,512]{1,0:T(8,128)(2,1)S(1)}, u32[]{:S(2)}, u32[]{:S(2)}) %collective-permute-start.20) | collective-permute-done | bytes 262176 | tf_op jit(solution)/shard_map/ppermute | solution.py:469
  126.6 4.6 %collective-permute-start.21 = (bf16[256,512]{1,0:T(8,128)(2,1)S(1)}, bf16[256,512]{1,0:T(8,128)(2,1)S(1)}, u32[]{:S(2)}, u32[]{:S(2)}) collective-permute-start(bf16[256,512]{1,0:T(8,128)(2,1)S(1)} %get-tuple-element.77.refs_2_), channel_id=1, source_target_pairs={{1,33},{3,35},{5,37},{7,39},{9,41},{11,43},{13,45},{15,47},{17,49}... | collective-permute-start | bytes 786440 | tf_op jit(solution)/shard_map/ppermute | solution.py:469
  132.1 5.7 %collective-permute-start.24 = (f32[128,256]{1,0:T(8,128)S(1)}, f32[128,256]{1,0:T(8,128)S(1)}, u32[]{:S(2)}, u32[]{:S(2)}) collective-permute-start(f32[128,256]{1,0:T(8,128)S(1)} %get-tuple-element.82.r_0_), channel_id=1, source_target_pairs={{1,9},{3,11},{5,13},{7,15},{9,1},{11,3},{13,5},{15,7},{17,25},{19,... | collective-permute-start | bytes 393224 | tf_op jit(solution)/shard_map/ppermute | solution.py:469
  138.4 3.2 %collective-permute-start.22 = (bf16[256,512]{1,0:T(8,128)(2,1)S(1)}, bf16[256,512]{1,0:T(8,128)(2,1)S(1)}, u32[]{:S(2)}, u32[]{:S(2)}) collective-permute-start(bf16[256,512]{1,0:T(8,128)(2,1)S(1)} %get-tuple-element.79.refs_2_), channel_id=1, source_target_pairs={{1,65},{3,67},{5,69},{7,71},{9,73},{11,75},{13,77},{15,79},{17,81}... | collective-permute-start | bytes 786440 | tf_op jit(solution)/shard_map/ppermute | solution.py:469
  142.0 3.1 %collective-permute-start.25 = (f32[128,256]{1,0:T(8,128)S(1)}, f32[128,256]{1,0:T(8,128)S(1)}, u32[]{:S(2)}, u32[]{:S(2)}) collective-permute-start(f32[128,256]{1,0:T(8,128)S(1)} %shard_map.97.r_0_), channel_id=1, source_target_pairs={{1,17},{3,19},{5,21},{7,23},{9,25},{11,27},{13,29},{15,31},{17,1},... | collective-permute-start | bytes 393224 | tf_op jit(solution)/shard_map/ppermute | solution.py:469
  146.4 4.8 %collective-permute-start.23 = (bf16[256,512]{1,0:T(8,128)(2,1)S(1)}, bf16[256,512]{1,0:T(8,128)(2,1)S(1)}, u32[]{:S(2)}, u32[]{:S(2)}) collective-permute-start(bf16[256,512]{1,0:T(8,128)(2,1)S(1)} %get-tuple-element.81.refs_2_), channel_id=1, source_target_pairs={{1,129},{3,131},{5,133},{7,135},{9,137},{11,139},{13,141},{15,143}... | collective-permute-start | bytes 786440 | tf_op jit(solution)/shard_map/ppermute | solution.py:469
  151.4 4.3 %collective-permute-start.26 = (f32[128,256]{1,0:T(8,128)S(1)}, f32[128,256]{1,0:T(8,128)S(1)}, u32[]{:S(2)}, u32[]{:S(2)}) collective-permute-start(f32[128,256]{1,0:T(8,128)S(1)} %shard_map.98.r_0_), channel_id=1, source_target_pairs={{1,33},{3,35},{5,37},{7,39},{9,41},{11,43},{13,45},{15,47},{17,49}... | collective-permute-start | bytes 393224 | tf_op jit(solution)/shard_map/ppermute | solution.py:469
  166.1 3.6 %collective-permute-start.28 = (f32[64,256]{1,0:T(8,128)S(1)}, f32[64,256]{1,0:T(8,128)S(1)}, u32[]{:S(2)}, u32[]{:S(2)}) collective-permute-start(f32[64,256]{1,0:T(8,128)S(1)} %slice_add_fusion), channel_id=1, source_target_pairs={{1,129},{3,131},{5,133},{7,135},{9,137},{11,139},{13,141},{15,143}... | collective-permute-start | bytes 196616 | tf_op jit(solution)/shard_map/ppermute | solution.py:469
  170.1 2.6 %collective-permute-done.28.refs_13_ = f32[64,256]{1,0:T(8,128)S(1)} collective-permute-done((f32[64,256]{1,0:T(8,128)S(1)}, f32[64,256]{1,0:T(8,128)S(1)}, u32[]{:S(2)}, u32[]{:S(2)}) %collective-permute-start.28) | collective-permute-done | bytes 65568 | tf_op jit(solution)/shard_map/ppermute | solution.py:469
  176.5 14.0 %collective-permute-done.7.odd_ref = f32[64,1280]{1,0:T(8,128)S(1)} collective-permute-done((f32[64,1280]{1,0:T(8,128)S(1)}, f32[64,1280]{1,0:T(8,128)S(1)}, u32[]{:S(2)}, u32[]{:S(2)}) %collective-permute-start.7) | collective-permute-done | bytes 327712 | tf_op jit(solution)/shard_map/ppermute | solution.py:469
  (116 shorter events, 56.9 us)
Async XLA Ops:
  3.9 7.7 %collective-permute-start = (bf16[1344,512]{1,0:T(8,128)(2,1)S(1)}, bf16[1344,512]{1,0:T(8,128)(2,1)}, u32[]{:S(2)}, u32[]{:S(2)}) collective-permute-start(bf16[1344,512]{1,0:T(8,128)(2,1)S(1)} %get-tuple-element.44.first), channel_id=1, source_target_pairs={{0,1},{1,0},{2,3},{3,2},{4,5},{5,4},{6,7},{7,6},{8,9},{9,8},{10,11... | collective-permute-start | bytes 4128776 | tf_op jit(solution)/shard_map/ppermute | solution.py:469
  11.7 32.2 %collective-permute-start.1 = (bf16[2688,512]{1,0:T(8,128)(2,1)}, bf16[2688,512]{1,0:T(8,128)(2,1)}, u32[]{:S(2)}, u32[]{:S(2)}) collective-permute-start(bf16[2688,512]{1,0:T(8,128)(2,1)} %shard_map.74.both.r_8_), channel_id=1, source_target_pairs={{0,2},{2,4},{4,6},{8,10},{10,12},{12,14},{16,18},{18,20},{20,22},{... | collective-permute-start | bytes 8257544 | tf_op jit(solution)/shard_map/ppermute | solution.py:469
  14.0 30.7 %collective-permute-start.2 = (bf16[2688,512]{1,0:T(8,128)(2,1)}, bf16[2688,512]{1,0:T(8,128)(2,1)}, u32[]{:S(2)}, u32[]{:S(2)}) collective-permute-start(bf16[2688,512]{1,0:T(8,128)(2,1)} %shard_map.74.both.r_8_), channel_id=1, source_target_pairs={{2,0},{4,2},{6,4},{10,8},{12,10},{14,12},{18,16},{20,18},{22,20},{... | collective-permute-start | bytes 8257544 | tf_op jit(solution)/shard_map/ppermute | solution.py:469
  19.0 13.7 %collective-permute-start.9 = (bf16[832,512]{1,0:T(8,128)(2,1)}, bf16[832,512]{1,0:T(8,128)(2,1)}, u32[]{:S(2)}, u32[]{:S(2)}) collective-permute-start(bf16[832,512]{1,0:T(8,128)(2,1)} %get-tuple-element.61), channel_id=1, source_target_pairs={{1,3},{3,1},{5,7},{7,5},{9,11},{11,9},{13,15},{15,13},{17,19},{19,... | collective-permute-start | bytes 2555912 | tf_op jit(solution)/shard_map/ppermute | solution.py:469
  38.0 12.5 %collective-permute-start.10 = (bf16[320,512]{1,0:T(8,128)(2,1)}, bf16[320,512]{1,0:T(8,128)(2,1)}, u32[]{:S(2)}, u32[]{:S(2)}) collective-permute-start(bf16[320,512]{1,0:T(8,128)(2,1)} %get-tuple-element.65), channel_id=1, source_target_pairs={{1,5},{3,7},{5,1},{7,3},{9,13},{11,15},{13,9},{15,11},{17,21},{19,... | collective-permute-start | bytes 983048 | tf_op jit(solution)/shard_map/ppermute | solution.py:469
  42.6 33.2 %collective-permute-start.16 = (bf16[256,512]{1,0:T(8,128)(2,1)S(1)}, bf16[256,512]{1,0:T(8,128)(2,1)S(1)}, u32[]{:S(2)}, u32[]{:S(2)}) collective-permute-start(bf16[256,512]{1,0:T(8,128)(2,1)S(1)} %shard_map.88.refs_2_), channel_id=1, source_target_pairs={{0,1},{2,3},{4,5},{6,7},{8,9},{10,11},{12,13},{14,15},{16,17},{18,... | collective-permute-start | bytes 786440 | tf_op jit(solution)/shard_map/ppermute | solution.py:469
  43.9 117.3 %collective-permute-start.3 = (bf16[2688,512]{1,0:T(8,128)(2,1)}, bf16[2688,512]{1,0:T(8,128)(2,1)S(1)}, u32[]{:S(2)}, u32[]{:S(2)}) collective-permute-start(bf16[2688,512]{1,0:T(8,128)(2,1)} %collective-permute-done.1.r_9_.right1), channel_id=1, source_target_pairs={{2,4},{4,6},{10,12},{12,14},{18,20},{20,22},{26,28},{28,30},{34,36... | collective-permute-start | bytes 8257544 | tf_op jit(solution)/shard_map/ppermute | solution.py:469
  44.7 116.4 %collective-permute-start.4 = (bf16[2688,512]{1,0:T(8,128)(2,1)}, bf16[2688,512]{1,0:T(8,128)(2,1)S(1)}, u32[]{:S(2)}, u32[]{:S(2)}) collective-permute-start(bf16[2688,512]{1,0:T(8,128)(2,1)} %collective-permute-done.2.r_10_.left1), channel_id=1, source_target_pairs={{2,0},{4,2},{10,8},{12,10},{18,16},{20,18},{26,24},{28,26},{34,32}... | collective-permute-start | bytes 8257544 | tf_op jit(solution)/shard_map/ppermute | solution.py:469
  53.3 27.1 %collective-permute-start.11 = (bf16[3,64,512]{2,1,0:T(8,128)(2,1)S(1)}, bf16[3,64,512]{2,1,0:T(8,128)(2,1)S(1)}, u32[]{:S(2)}, u32[]{:S(2)}) collective-permute-start(bf16[3,64,512]{2,1,0:T(8,128)(2,1)S(1)} %get-tuple-element.67.held_ref), channel_id=1, source_target_pairs={{1,9},{3,11},{5,13},{7,15},{9,1},{11,3},{13,5},{15,7},{17,25},{19,... | collective-permute-start | bytes 589832 | tf_op jit(solution)/shard_map/ppermute | solution.py:469
  76.1 11.2 %collective-permute-start.17 = (bf16[256,512]{1,0:T(8,128)(2,1)S(1)}, bf16[256,512]{1,0:T(8,128)(2,1)S(1)}, u32[]{:S(2)}, u32[]{:S(2)}) collective-permute-start(bf16[256,512]{1,0:T(8,128)(2,1)S(1)} %shard_map.89.refs_2_), channel_id=1, source_target_pairs={{1,3},{3,1},{5,7},{7,5},{9,11},{11,9},{13,15},{15,13},{17,19},{19,... | collective-permute-start | bytes 786440 | tf_op jit(solution)/shard_map/ppermute | solution.py:469
  80.5 12.2 %collective-permute-start.12 = (bf16[2,64,512]{2,1,0:T(8,128)(2,1)S(1)}, bf16[2,64,512]{2,1,0:T(8,128)(2,1)S(1)}, u32[]{:S(2)}, u32[]{:S(2)}) collective-permute-start(bf16[2,64,512]{2,1,0:T(8,128)(2,1)S(1)} %get-tuple-element.69.held_ref), channel_id=1, source_target_pairs={{1,17},{3,19},{5,21},{7,23},{9,25},{11,27},{13,29},{15,31},{17,1},... | collective-permute-start | bytes 393224 | tf_op jit(solution)/shard_map/ppermute | solution.py:469
  87.7 13.4 %collective-permute-start.18 = (bf16[256,512]{1,0:T(8,128)(2,1)S(1)}, bf16[256,512]{1,0:T(8,128)(2,1)S(1)}, u32[]{:S(2)}, u32[]{:S(2)}) collective-permute-start(bf16[256,512]{1,0:T(8,128)(2,1)S(1)} %shard_map.90.refs_2_), channel_id=1, source_target_pairs={{1,5},{3,7},{5,1},{7,3},{9,13},{11,15},{13,9},{15,11},{17,21},{19,... | collective-permute-start | bytes 786440 | tf_op jit(solution)/shard_map/ppermute | solution.py:469
  99.2 16.7 %collective-permute-start.14 = (bf16[4,64,512]{2,1,0:T(8,128)(2,1)S(1)}, bf16[4,64,512]{2,1,0:T(8,128)(2,1)S(1)}, u32[]{:S(2)}, u32[]{:S(2)}) collective-permute-start(bf16[4,64,512]{2,1,0:T(8,128)(2,1)S(1)} %shard_map.85.r_1_), channel_id=1, source_target_pairs={{1,5},{3,7},{5,1},{7,3},{9,13},{11,15},{13,9},{15,11},{17,21},{19,... | collective-permute-start | bytes 786440 | tf_op jit(solution)/shard_map/ppermute | solution.py:469
  101.5 16.4 %collective-permute-start.19 = (bf16[256,512]{1,0:T(8,128)(2,1)S(1)}, bf16[256,512]{1,0:T(8,128)(2,1)S(1)}, u32[]{:S(2)}, u32[]{:S(2)}) collective-permute-start(bf16[256,512]{1,0:T(8,128)(2,1)S(1)} %shard_map.91.refs_2_), channel_id=1, source_target_pairs={{1,9},{3,11},{5,13},{7,15},{9,1},{11,3},{13,5},{15,7},{17,25},{19,... | collective-permute-start | bytes 786440 | tf_op jit(solution)/shard_map/ppermute | solution.py:469
  116.0 15.8 %collective-permute-start.15 = (bf16[4,128,512]{2,1,0:T(8,128)(2,1)S(1)}, bf16[4,128,512]{2,1,0:T(8,128)(2,1)S(1)}, u32[]{:S(2)}, u32[]{:S(2)}) collective-permute-start(bf16[4,128,512]{2,1,0:T(8,128)(2,1)S(1)} %shard_map.86.r_1_), channel_id=1, source_target_pairs={{1,3},{3,1},{5,7},{7,5},{9,11},{11,9},{13,15},{15,13},{17,19},{19,... | collective-permute-start | bytes 1572872 | tf_op jit(solution)/shard_map/ppermute | solution.py:469
  118.6 7.4 %collective-permute-start.20 = (bf16[256,512]{1,0:T(8,128)(2,1)S(1)}, bf16[256,512]{1,0:T(8,128)(2,1)S(1)}, u32[]{:S(2)}, u32[]{:S(2)}) collective-permute-start(bf16[256,512]{1,0:T(8,128)(2,1)S(1)} %get-tuple-element.75.refs_2_), channel_id=1, source_target_pairs={{1,17},{3,19},{5,21},{7,23},{9,25},{11,27},{13,29},{15,31},{17,1},... | collective-permute-start | bytes 786440 | tf_op jit(solution)/shard_map/ppermute | solution.py:469
  126.6 11.2 %collective-permute-start.21 = (bf16[256,512]{1,0:T(8,128)(2,1)S(1)}, bf16[256,512]{1,0:T(8,128)(2,1)S(1)}, u32[]{:S(2)}, u32[]{:S(2)}) collective-permute-start(bf16[256,512]{1,0:T(8,128)(2,1)S(1)} %get-tuple-element.77.refs_2_), channel_id=1, source_target_pairs={{1,33},{3,35},{5,37},{7,39},{9,41},{11,43},{13,45},{15,47},{17,49}... | collective-permute-start | bytes 786440 | tf_op jit(solution)/shard_map/ppermute | solution.py:469
  132.1 9.7 %collective-permute-start.24 = (f32[128,256]{1,0:T(8,128)S(1)}, f32[128,256]{1,0:T(8,128)S(1)}, u32[]{:S(2)}, u32[]{:S(2)}) collective-permute-start(f32[128,256]{1,0:T(8,128)S(1)} %get-tuple-element.82.r_0_), channel_id=1, source_target_pairs={{1,9},{3,11},{5,13},{7,15},{9,1},{11,3},{13,5},{15,7},{17,25},{19,... | collective-permute-start | bytes 393224 | tf_op jit(solution)/shard_map/ppermute | solution.py:469
  138.4 7.4 %collective-permute-start.22 = (bf16[256,512]{1,0:T(8,128)(2,1)S(1)}, bf16[256,512]{1,0:T(8,128)(2,1)S(1)}, u32[]{:S(2)}, u32[]{:S(2)}) collective-permute-start(bf16[256,512]{1,0:T(8,128)(2,1)S(1)} %get-tuple-element.79.refs_2_), channel_id=1, source_target_pairs={{1,65},{3,67},{5,69},{7,71},{9,73},{11,75},{13,77},{15,79},{17,81}... | collective-permute-start | bytes 786440 | tf_op jit(solution)/shard_map/ppermute | solution.py:469
  142.0 9.2 %collective-permute-start.25 = (f32[128,256]{1,0:T(8,128)S(1)}, f32[128,256]{1,0:T(8,128)S(1)}, u32[]{:S(2)}, u32[]{:S(2)}) collective-permute-start(f32[128,256]{1,0:T(8,128)S(1)} %shard_map.97.r_0_), channel_id=1, source_target_pairs={{1,17},{3,19},{5,21},{7,23},{9,25},{11,27},{13,29},{15,31},{17,1},... | collective-permute-start | bytes 393224 | tf_op jit(solution)/shard_map/ppermute | solution.py:469
  146.4 23.3 %collective-permute-start.23 = (bf16[256,512]{1,0:T(8,128)(2,1)S(1)}, bf16[256,512]{1,0:T(8,128)(2,1)S(1)}, u32[]{:S(2)}, u32[]{:S(2)}) collective-permute-start(bf16[256,512]{1,0:T(8,128)(2,1)S(1)} %get-tuple-element.81.refs_2_), channel_id=1, source_target_pairs={{1,129},{3,131},{5,133},{7,135},{9,137},{11,139},{13,141},{15,143}... | collective-permute-start | bytes 786440 | tf_op jit(solution)/shard_map/ppermute | solution.py:469
  161.9 14.6 %collective-permute-start.5 = (f32[64,1280]{1,0:T(8,128)S(1)}, f32[64,1280]{1,0:T(8,128)S(1)}, u32[]{:S(2)}, u32[]{:S(2)}) collective-permute-start(f32[64,1280]{1,0:T(8,128)S(1)} %pad_maximum_fusion), channel_id=1, source_target_pairs={{0,1},{2,3},{4,5},{6,7},{8,9},{10,11},{12,13},{14,15},{16,17},{18,... | collective-permute-start | bytes 983048 | tf_op jit(solution)/shard_map/ppermute | solution.py:469
  163.9 12.6 %collective-permute-start.6 = (f32[64,1280]{1,0:T(8,128)S(1)}, f32[64,1280]{1,0:T(8,128)S(1)}, u32[]{:S(2)}, u32[]{:S(2)}) collective-permute-start(f32[64,1280]{1,0:T(8,128)S(1)} %get-tuple-element.84), channel_id=1, source_target_pairs={{2,0},{4,6},{10,8},{12,14},{18,16},{20,22},{26,24},{28,30},{34,32}... | collective-permute-start | bytes 983048 | tf_op jit(solution)/shard_map/ppermute | solution.py:469
  164.7 25.8 %collective-permute-start.7 = (f32[64,1280]{1,0:T(8,128)S(1)}, f32[64,1280]{1,0:T(8,128)S(1)}, u32[]{:S(2)}, u32[]{:S(2)}) collective-permute-start(f32[64,1280]{1,0:T(8,128)S(1)} %get-tuple-element.83), channel_id=1, source_target_pairs={{2,1},{4,7},{10,9},{12,15},{18,17},{20,23},{26,25},{28,31},{34,33}... | collective-permute-start | bytes 983048 | tf_op jit(solution)/shard_map/ppermute | solution.py:469
  (27 other events, 216.4 us)
